TPU v7x, 512 devices: a whole 4x8x8 slice. The times are simulated.
512 devices in a mesh: dp: 32 (over z_lo, y, core), expert: 16 (over x, z_hi).
Axes of the slice: x: 4, y: 8, z: 8 (z_hi: 4, z_lo: 2; z = z_hi * 2 + z_lo), core: 2. Of those that a mesh axis runs over, the one named last changes fastest.
Arguments:
- grad_out: bfloat16 [4, 32768, 1024], P(None, ('dp', 'expert')), may hold values from -12 to 12
- routes: int32 [4, 32768, 8], P(None, ('dp', 'expert')), may hold values from 0 to 127, all different within a row; in each aligned block of 64 rows (0 to 63, 64 to 127, ..., all dimensions but the last counted through in order) at most 8 rows name the same one
- route_probs: bfloat16 [4, 32768, 8], P(None, ('dp', 'expert')), may hold values from 0.049804688 to 0.3984375
- dispatched: bfloat16 [4, 65536, 1024], P(None, ('dp', 'expert')), may hold values from -12 to 12, as said below
- w_gate: bfloat16 [1024, 4096], P(None, 'expert'), may hold values from -0.1875 to 0.1875
- w_up: bfloat16 [1024, 4096], P(None, 'expert'), may hold values from -0.1875 to 0.1875
- w_down: bfloat16 [4096, 1024], P('expert'), may hold values from -0.25 to 0.25
Outputs:
- grad_in: bfloat16 [4, 32768, 1024], P(None, ('dp', 'expert'))
- grad_gate: float32 [1024, 4096], P('dp', 'expert')
- grad_up: float32 [1024, 4096], P('dp', 'expert')
- grad_down_t: float32 [1024, 4096], P('dp', 'expert')
Inputs may be any that keep to these rules, and one draw needn't show every extreme that they name: `routes`: in each micro-batch, among the 64 rows of one device no expert is named more than 8 times, a bound that some expert reaches in some of these blocks. `dispatched`: within each group of 16 consecutive blocks of 128 rows, blocks 2e and 2e + 1 are equal.
All inputs are finite; a program needn't handle non-finite values.
Results may differ from a plain program's by a relative error of at most 0.0058.
Values may be sent and summed in bfloat16 or wider, within the bound.
A program may use at most 64 MiB of HBM per device.

v0:
```python
import jax
import jax.numpy as jnp
from jax import lax
from jax.sharding import PartitionSpec as P

TOPK = 8
CAPS = 8


def swapped(x, axis, stride):
    return lax.ppermute(x, axis, [(i, i ^ 1 << stride) for i in range(lax.axis_size(axis))])


def in_one_piece(arrays, axis, dim, along):
    widths = [a.shape[along] for a in arrays]
    both = jnp.concatenate(arrays, axis=along)
    filled = lax.psum_scatter(both, axis, scatter_dimension=dim, tiled=True)
    return tuple(jnp.split(filled, [sum(widths[:k]) for k in range(1, len(widths))], axis=along))


def slot_take(route_ids, targets, flat_dy, flat_probs, capacity):
    hitting = (route_ids == targets[:, None]).astype(jnp.int32)
    ranking = jnp.cumsum(hitting, axis=1) - 1
    chosen = hitting[:, None, :] * (
        ranking[:, None, :] == jnp.arange(capacity, dtype=jnp.int32)[None, :, None]
    ).astype(jnp.int32)
    position = jnp.sum(
        chosen * jnp.arange(route_ids.shape[1], dtype=jnp.int32)[None, None, :], axis=2
    )
    living = jnp.sum(chosen, axis=2) > 0
    weights = jnp.take_along_axis(flat_probs, position, axis=1)
    rows_at = position // TOPK
    picked = jnp.take(flat_dy, rows_at.reshape(-1), axis=0)
    scaled = (weights.reshape(-1, 1).astype(jnp.float32) * picked.astype(jnp.float32)).astype(
        jnp.bfloat16
    )
    return jnp.where(living.reshape(-1, 1), scaled, jnp.zeros_like(scaled))


def contract_rows(left, right):
    return lax.dot_general(
        left, right, (((0,), (0,)), ((), ())), preferred_element_type=jnp.float32
    )


def contract_cols(left, right):
    return lax.dot_general(
        left, right, (((1,), (1,)), ((), ())), preferred_element_type=jnp.float32
    )


def per_device(grad_out, routes, route_probs, dispatched, w_gate, w_up, w_down):
    groups = lax.axis_size("expert")
    member = lax.axis_index("expert")
    window = groups // 2
    tok_dev = grad_out.shape[1]
    model_width = grad_out.shape[2]
    half_cols = w_gate.shape[1]
    capacity = CAPS
    half_caps = capacity // 2
    slot_count = groups * capacity
    parity = member % 2
    acc_gate = jnp.zeros((model_width, half_cols), jnp.float32)
    acc_up = jnp.zeros((model_width, half_cols), jnp.float32)
    acc_down = jnp.zeros((model_width, half_cols), jnp.float32)
    outputs = []
    for micro_idx in range(grad_out.shape[0]):
        own_ids = routes[micro_idx]
        targets = jnp.arange(window, dtype=jnp.int32)
        flat_ids = jnp.broadcast_to(own_ids.reshape(1, -1), (window, tok_dev * TOPK))
        flat_probs = jnp.broadcast_to(
            route_probs[micro_idx].reshape(1, -1), (window, tok_dev * TOPK)
        )
        sending = slot_take(flat_ids, targets, grad_out[micro_idx], flat_probs, capacity)
        arrived = lax.all_to_all(
            sending.reshape(groups, half_caps, model_width),
            "expert",
            split_axis=0,
            concat_axis=0,
            tiled=True,
        )
        partner_rows = swapped(arrived, "expert", 0)
        lower = jnp.where(parity == 0, arrived, partner_rows)
        upper = jnp.where(parity == 0, partner_rows, arrived)
        scaled = jnp.concatenate([lower, upper], axis=1).reshape(slot_count, model_width)
        inputs = dispatched[micro_idx]
        gate_pre = jnp.dot(inputs, w_gate, preferred_element_type=jnp.float32)
        up_pre = jnp.dot(inputs, w_up, preferred_element_type=jnp.float32)
        sigmoid = jax.nn.sigmoid(gate_pre)
        activated = gate_pre * sigmoid
        hidden = (activated * up_pre).astype(jnp.bfloat16)
        acc_down = acc_down + contract_rows(scaled, hidden)
        dhidden = contract_cols(scaled, w_down)
        d_gate = (dhidden * up_pre * sigmoid * (1.0 + gate_pre * (1.0 - sigmoid))).astype(
            jnp.bfloat16
        )
        d_up = (dhidden * activated).astype(jnp.bfloat16)
        acc_gate = acc_gate + contract_rows(inputs, d_gate)
        acc_up = acc_up + contract_rows(inputs, d_up)
        partial_value = contract_cols(d_gate, w_gate) + contract_cols(d_up, w_up)
        blocks = partial_value.reshape(groups, half_caps, 2, model_width)
        kept_part = lax.dynamic_index_in_dim(blocks, parity, 2, keepdims=False)
        given_part = lax.dynamic_index_in_dim(blocks, 1 - parity, 2, keepdims=False)
        partner = swapped(given_part, "expert", 0)
        returned = lax.all_to_all(
            kept_part + partner, "expert", split_axis=0, concat_axis=0, tiled=True
        )
        summed = jnp.swapaxes(returned.reshape(window, 2, half_caps, model_width), 1, 2).reshape(
            window, capacity, model_width
        )
        inside = own_ids < window
        hitting = (
            own_ids.reshape(-1)[:, None] == jnp.arange(window, dtype=jnp.int32)[None, :]
        ).astype(jnp.int32)
        ranking = jnp.sum((jnp.cumsum(hitting, axis=0) - 1) * hitting, axis=1).reshape(
            tok_dev, TOPK
        )
        slot_keys = jnp.where(inside, own_ids * capacity + ranking, -1)
        mixing = jnp.sum(
            (
                slot_keys[:, :, None]
                == jnp.arange(window * capacity, dtype=jnp.int32)[None, None, :]
            ).astype(jnp.float32),
            axis=1,
        )
        grad_tokens = jnp.dot(
            mixing,
            summed.reshape(window * capacity, model_width),
            precision=lax.Precision.HIGHEST,
            preferred_element_type=jnp.float32,
        )
        outputs.append(grad_tokens.astype(jnp.bfloat16))
    reduced = in_one_piece((acc_gate, acc_up, acc_down), "dp", 0, 1)
    factor = 1.0 / (grad_out.shape[0] * lax.axis_size("dp"))
    return (jnp.stack(outputs), reduced[0] * factor, reduced[1] * factor, reduced[2] * factor)


def solution(mesh):
    return jax.shard_map(
        per_device,
        mesh=mesh,
        in_specs=(
            P(None, ("dp", "expert"), None),
            P(None, ("dp", "expert"), None),
            P(None, ("dp", "expert"), None),
            P(None, ("dp", "expert"), None),
            P(None, "expert"),
            P(None, "expert"),
            P("expert", None),
        ),
        out_specs=(
            P(None, ("dp", "expert"), None),
            P("dp", "expert"),
            P("dp", "expert"),
            P("dp", "expert"),
        ),
        check_vma=False,
    )
```

profile of v0, /device:TPU:4, one launch (start us, length us, event | category | flops | bytes accessed | tf_op | source)
XLA Modules:
  0.0 256.2 jit_solution(15513255890719942221)
XLA Ops:
  17.7 13.3 %all-to-all-start.2 = ((bf16[16,4,1024]{2,1,0:T(4,128)(2,1)}), bf16[16,4,1024]{2,1,0:T(4,128)(2,1)S(1)}, u32[]{:S(2)}, u32[]{:S(2)}) async-start(bf16[16,4,1024]{2,1,0:T(4,128)(2,1)} %reshape.509), calls=%async_computation.2 | async-start | bytes 262144 | tf_op jit(solution)/shard_map/all_to_all | solution.py:75
  46.3 9.6 %all-to-all-start.6 = ((bf16[16,4,1024]{2,1,0:T(4,128)(2,1)}), bf16[16,4,1024]{2,1,0:T(4,128)(2,1)S(1)}, u32[]{:S(2)}, u32[]{:S(2)}) async-start(bf16[16,4,1024]{2,1,0:T(4,128)(2,1)} %reshape.521), calls=%async_computation.6 | async-start | bytes 262144 | tf_op jit(solution)/shard_map/all_to_all | solution.py:75
  56.2 8.2 %all-to-all-done.6 = bf16[16,4,1024]{2,1,0:T(4,128)(2,1)S(1)} async-done(((bf16[16,4,1024]{2,1,0:T(4,128)(2,1)}), bf16[16,4,1024]{2,1,0:T(4,128)(2,1)S(1)}, u32[]{:S(2)}, u32[]{:S(2)}) %all-to-all-start.6) | async-done | bytes 131104 | tf_op jit(solution)/shard_map/all_to_all | solution.py:75
  64.4 6.0 %all-to-all-start.4 = ((bf16[16,4,1024]{2,1,0:T(4,128)(2,1)}), bf16[16,4,1024]{2,1,0:T(4,128)(2,1)S(1)}, u32[]{:S(2)}, u32[]{:S(2)}) async-start(bf16[16,4,1024]{2,1,0:T(4,128)(2,1)} %reshape.515), calls=%async_computation.4 | async-start | bytes 262144 | tf_op jit(solution)/shard_map/all_to_all | solution.py:75
  70.7 4.3 %collective-permute-start.2 = (bf16[16,4,1024]{2,1,0:T(4,128)(2,1)S(1)}, bf16[16,4,1024]{2,1,0:T(4,128)(2,1)}, u32[]{:S(2)}, u32[]{:S(2)}) collective-permute-start(bf16[16,4,1024]{2,1,0:T(4,128)(2,1)S(1)} %all-to-all-done.2), channel_id=1, source_target_pairs={{0,1},{1,0},{2,3},{3,2},{4,5},{5,4},{6,7},{7,6},{8,9},{9,8},{10,11... | collective-permute-start | bytes 393224 | tf_op jit(solution)/shard_map/ppermute | solution.py:11
  74.9 4.4 %all-to-all-done.4 = bf16[16,4,1024]{2,1,0:T(4,128)(2,1)S(1)} async-done(((bf16[16,4,1024]{2,1,0:T(4,128)(2,1)}), bf16[16,4,1024]{2,1,0:T(4,128)(2,1)S(1)}, u32[]{:S(2)}, u32[]{:S(2)}) %all-to-all-start.4) | async-done | bytes 131104 | tf_op jit(solution)/shard_map/all_to_all | solution.py:75
  79.4 6.7 %all-to-all-start = ((bf16[16,4,1024]{2,1,0:T(4,128)(2,1)}), bf16[16,4,1024]{2,1,0:T(4,128)(2,1)}, u32[]{:S(2)}, u32[]{:S(2)}) async-start(bf16[16,4,1024]{2,1,0:T(4,128)(2,1)} %reshape.503), calls=%async_computation | async-start | bytes 262144 | tf_op jit(solution)/shard_map/all_to_all | solution.py:75
  86.3 4.3 %collective-permute-start.4 = (bf16[16,4,1024]{2,1,0:T(4,128)(2,1)S(1)}, bf16[16,4,1024]{2,1,0:T(4,128)(2,1)}, u32[]{:S(2)}, u32[]{:S(2)}) collective-permute-start(bf16[16,4,1024]{2,1,0:T(4,128)(2,1)S(1)} %all-to-all-done.4), channel_id=1, source_target_pairs={{0,1},{1,0},{2,3},{3,2},{4,5},{5,4},{6,7},{7,6},{8,9},{9,8},{10,11... | collective-permute-start | bytes 393224 | tf_op jit(solution)/shard_map/ppermute | solution.py:11
  90.6 2.5 collective-permute-start.6
  94.4 3.9 %collective-permute-start = (bf16[16,4,1024]{2,1,0:T(4,128)(2,1)}, bf16[16,4,1024]{2,1,0:T(4,128)(2,1)S(1)}, u32[]{:S(2)}, u32[]{:S(2)}) collective-permute-start(bf16[16,4,1024]{2,1,0:T(4,128)(2,1)} %all-to-all-done), channel_id=1, source_target_pairs={{0,1},{1,0},{2,3},{3,2},{4,5},{5,4},{6,7},{7,6},{8,9},{9,8},{10,11... | collective-permute-start | bytes 393224 | tf_op jit(solution)/shard_map/ppermute | solution.py:11
  102.0 3.9 %collective-permute-done = bf16[16,4,1024]{2,1,0:T(4,128)(2,1)S(1)} collective-permute-done((bf16[16,4,1024]{2,1,0:T(4,128)(2,1)}, bf16[16,4,1024]{2,1,0:T(4,128)(2,1)S(1)}, u32[]{:S(2)}, u32[]{:S(2)}) %collective-permute-start) | collective-permute-done | bytes 131104 | tf_op jit(solution)/shard_map/ppermute | solution.py:11
  114.8 3.5 %copy.78 = f32[1024,768]{1,0:T(8,128)} copy(f32[1024,768]{0,1:T(8,128)} %pad_maximum_fusion) | data formatting | bytes 6291456
  127.5 4.8 %collective-permute-start.3 = (f32[16,4,1024]{2,1,0:T(4,128)}, f32[16,4,1024]{2,1,0:T(4,128)}, u32[]{:S(2)}, u32[]{:S(2)}) collective-permute-start(f32[16,4,1024]{2,1,0:T(4,128)} %bitcast.223), channel_id=1, source_target_pairs={{0,1},{1,0},{2,3},{3,2},{4,5},{5,4},{6,7},{7,6},{8,9},{9,8},{10,11... | collective-permute-start | bytes 786440 | tf_op jit(solution)/shard_map/ppermute | solution.py:11
  136.5 14.3 %collective-permute-done.1 = f32[16,4,1024]{2,1,0:T(4,128)} collective-permute-done((f32[16,4,1024]{2,1,0:T(4,128)}, f32[16,4,1024]{2,1,0:T(4,128)}, u32[]{:S(2)}, u32[]{:S(2)}) %collective-permute-start.1) | collective-permute-done | bytes 262176 | tf_op jit(solution)/shard_map/ppermute | solution.py:11
  152.5 8.1 %all-to-all-start.1 = ((f32[16,4,1024]{2,1,0:T(4,128)}), f32[16,4,1024]{2,1,0:T(4,128)S(1)}, u32[]{:S(2)}, u32[]{:S(2)}) async-start(f32[16,4,1024]{2,1,0:T(4,128)} %bitcast_add_fusion.3), calls=%async_computation.1 | async-start | bytes 524288 | tf_op jit(solution)/shard_map/all_to_all | solution.py:105
  162.7 10.0 %all-to-all-done.1 = f32[16,4,1024]{2,1,0:T(4,128)S(1)} async-done(((f32[16,4,1024]{2,1,0:T(4,128)}), f32[16,4,1024]{2,1,0:T(4,128)S(1)}, u32[]{:S(2)}, u32[]{:S(2)}) %all-to-all-start.1) | async-done | bytes 262176 | tf_op jit(solution)/shard_map/all_to_all | solution.py:105
  172.7 6.7 %all-to-all-start.3 = ((f32[16,4,1024]{2,1,0:T(4,128)}), f32[16,4,1024]{2,1,0:T(4,128)S(1)}, u32[]{:S(2)}, u32[]{:S(2)}) async-start(f32[16,4,1024]{2,1,0:T(4,128)} %bitcast_add_fusion.2), calls=%async_computation.3 | async-start | bytes 524288 | tf_op jit(solution)/shard_map/all_to_all | solution.py:105
  180.8 4.3 %collective-permute-start.5 = (f32[16,4,1024]{2,1,0:T(4,128)S(1)}, f32[16,4,1024]{2,1,0:T(4,128)S(1)}, u32[]{:S(2)}, u32[]{:S(2)}) collective-permute-start(f32[16,4,1024]{2,1,0:T(4,128)S(1)} %bitcast.264), channel_id=1, source_target_pairs={{0,1},{1,0},{2,3},{3,2},{4,5},{5,4},{6,7},{7,6},{8,9},{9,8},{10,11... | collective-permute-start | bytes 786440 | tf_op jit(solution)/shard_map/ppermute | solution.py:11
  185.9 5.5 %all-to-all-done.3 = f32[16,4,1024]{2,1,0:T(4,128)S(1)} async-done(((f32[16,4,1024]{2,1,0:T(4,128)}), f32[16,4,1024]{2,1,0:T(4,128)S(1)}, u32[]{:S(2)}, u32[]{:S(2)}) %all-to-all-start.3) | async-done | bytes 262176 | tf_op jit(solution)/shard_map/all_to_all | solution.py:105
  191.3 6.1 %all-to-all-start.7 = ((f32[16,4,1024]{2,1,0:T(4,128)}), f32[16,4,1024]{2,1,0:T(4,128)S(1)}, u32[]{:S(2)}, u32[]{:S(2)}) async-start(f32[16,4,1024]{2,1,0:T(4,128)} %bitcast_add_fusion), calls=%async_computation.7 | async-start | bytes 524288 | tf_op jit(solution)/shard_map/all_to_all | solution.py:105
  200.7 9.2 %all-to-all-done.7 = f32[16,4,1024]{2,1,0:T(4,128)S(1)} async-done(((f32[16,4,1024]{2,1,0:T(4,128)}), f32[16,4,1024]{2,1,0:T(4,128)S(1)}, u32[]{:S(2)}, u32[]{:S(2)}) %all-to-all-start.7) | async-done | bytes 262176 | tf_op jit(solution)/shard_map/all_to_all | solution.py:105
  209.9 6.6 %all-to-all-start.5 = ((f32[16,4,1024]{2,1,0:T(4,128)}), f32[16,4,1024]{2,1,0:T(4,128)S(1)}, u32[]{:S(2)}, u32[]{:S(2)}) async-start(f32[16,4,1024]{2,1,0:T(4,128)} %bitcast_add_fusion.1), calls=%async_computation.5 | async-start | bytes 524288 | tf_op jit(solution)/shard_map/all_to_all | solution.py:105
  218.3 9.8 %all-to-all-done.5 = f32[16,4,1024]{2,1,0:T(4,128)S(1)} async-done(((f32[16,4,1024]{2,1,0:T(4,128)}), f32[16,4,1024]{2,1,0:T(4,128)S(1)}, u32[]{:S(2)}, u32[]{:S(2)}) %all-to-all-start.5) | async-done | bytes 262176 | tf_op jit(solution)/shard_map/all_to_all | solution.py:105
  230.8 15.3 %reduce-scatter.4.cloned.1.call-done = f32[32,768]{1,0:T(8,128)} async-done(((f32[1024,768]{1,0:T(8,128)}), f32[32,768]{1,0:T(8,128)}) %reduce-scatter.4.cloned.1.call-update) | async-done | bytes 98320
  (299 shorter events, 69.6 us)
Async XLA Ops:
  17.7 28.6 %all-to-all-start.2 = ((bf16[16,4,1024]{2,1,0:T(4,128)(2,1)}), bf16[16,4,1024]{2,1,0:T(4,128)(2,1)S(1)}, u32[]{:S(2)}, u32[]{:S(2)}) async-start(bf16[16,4,1024]{2,1,0:T(4,128)(2,1)} %reshape.509), calls=%async_computation.2 | async-start | bytes 262144 | tf_op jit(solution)/shard_map/all_to_all | solution.py:75
  46.3 18.1 %all-to-all-start.6 = ((bf16[16,4,1024]{2,1,0:T(4,128)(2,1)}), bf16[16,4,1024]{2,1,0:T(4,128)(2,1)S(1)}, u32[]{:S(2)}, u32[]{:S(2)}) async-start(bf16[16,4,1024]{2,1,0:T(4,128)(2,1)} %reshape.521), calls=%async_computation.6 | async-start | bytes 262144 | tf_op jit(solution)/shard_map/all_to_all | solution.py:75
  64.4 15.0 %all-to-all-start.4 = ((bf16[16,4,1024]{2,1,0:T(4,128)(2,1)}), bf16[16,4,1024]{2,1,0:T(4,128)(2,1)S(1)}, u32[]{:S(2)}, u32[]{:S(2)}) async-start(bf16[16,4,1024]{2,1,0:T(4,128)(2,1)} %reshape.515), calls=%async_computation.4 | async-start | bytes 262144 | tf_op jit(solution)/shard_map/all_to_all | solution.py:75
  70.7 27.6 %collective-permute-start.2 = (bf16[16,4,1024]{2,1,0:T(4,128)(2,1)S(1)}, bf16[16,4,1024]{2,1,0:T(4,128)(2,1)}, u32[]{:S(2)}, u32[]{:S(2)}) collective-permute-start(bf16[16,4,1024]{2,1,0:T(4,128)(2,1)S(1)} %all-to-all-done.2), channel_id=1, source_target_pairs={{0,1},{1,0},{2,3},{3,2},{4,5},{5,4},{6,7},{7,6},{8,9},{9,8},{10,11... | collective-permute-start | bytes 393224 | tf_op jit(solution)/shard_map/ppermute | solution.py:11
  79.4 15.0 %all-to-all-start = ((bf16[16,4,1024]{2,1,0:T(4,128)(2,1)}), bf16[16,4,1024]{2,1,0:T(4,128)(2,1)}, u32[]{:S(2)}, u32[]{:S(2)}) async-start(bf16[16,4,1024]{2,1,0:T(4,128)(2,1)} %reshape.503), calls=%async_computation | async-start | bytes 262144 | tf_op jit(solution)/shard_map/all_to_all | solution.py:75
  86.0 160.1 %reduce-scatter.4.cloned.1.call-start = ((), (), s32[]{:S(2)}) async-start(), calls=%async_computation.9 | async-start | bytes 3244032
  86.3 14.7 %collective-permute-start.4 = (bf16[16,4,1024]{2,1,0:T(4,128)(2,1)S(1)}, bf16[16,4,1024]{2,1,0:T(4,128)(2,1)}, u32[]{:S(2)}, u32[]{:S(2)}) collective-permute-start(bf16[16,4,1024]{2,1,0:T(4,128)(2,1)S(1)} %all-to-all-done.4), channel_id=1, source_target_pairs={{0,1},{1,0},{2,3},{3,2},{4,5},{5,4},{6,7},{7,6},{8,9},{9,8},{10,11... | collective-permute-start | bytes 393224 | tf_op jit(solution)/shard_map/ppermute | solution.py:11
  90.6 17.8 %collective-permute-start.6 = (bf16[16,4,1024]{2,1,0:T(4,128)(2,1)S(1)}, bf16[16,4,1024]{2,1,0:T(4,128)(2,1)}, u32[]{:S(2)}, u32[]{:S(2)}) collective-permute-start(bf16[16,4,1024]{2,1,0:T(4,128)(2,1)S(1)} %all-to-all-done.6), channel_id=1, source_target_pairs={{0,1},{1,0},{2,3},{3,2},{4,5},{5,4},{6,7},{7,6},{8,9},{9,8},{10,11... | collective-permute-start | bytes 393224 | tf_op jit(solution)/shard_map/ppermute | solution.py:11
  94.4 11.6 %collective-permute-start = (bf16[16,4,1024]{2,1,0:T(4,128)(2,1)}, bf16[16,4,1024]{2,1,0:T(4,128)(2,1)S(1)}, u32[]{:S(2)}, u32[]{:S(2)}) collective-permute-start(bf16[16,4,1024]{2,1,0:T(4,128)(2,1)} %all-to-all-done), channel_id=1, source_target_pairs={{0,1},{1,0},{2,3},{3,2},{4,5},{5,4},{6,7},{7,6},{8,9},{9,8},{10,11... | collective-permute-start | bytes 393224 | tf_op jit(solution)/shard_map/ppermute | solution.py:11
  123.3 27.5 %collective-permute-start.1 = (f32[16,4,1024]{2,1,0:T(4,128)}, f32[16,4,1024]{2,1,0:T(4,128)}, u32[]{:S(2)}, u32[]{:S(2)}) collective-permute-start(f32[16,4,1024]{2,1,0:T(4,128)} %bitcast.224), channel_id=1, source_target_pairs={{0,1},{1,0},{2,3},{3,2},{4,5},{5,4},{6,7},{7,6},{8,9},{9,8},{10,11... | collective-permute-start | bytes 786440 | tf_op jit(solution)/shard_map/ppermute | solution.py:11
  127.5 33.5 %collective-permute-start.3 = (f32[16,4,1024]{2,1,0:T(4,128)}, f32[16,4,1024]{2,1,0:T(4,128)}, u32[]{:S(2)}, u32[]{:S(2)}) collective-permute-start(f32[16,4,1024]{2,1,0:T(4,128)} %bitcast.223), channel_id=1, source_target_pairs={{0,1},{1,0},{2,3},{3,2},{4,5},{5,4},{6,7},{7,6},{8,9},{9,8},{10,11... | collective-permute-start | bytes 786440 | tf_op jit(solution)/shard_map/ppermute | solution.py:11
  134.6 50.5 %collective-permute-start.7 = (f32[16,4,1024]{2,1,0:T(4,128)}, f32[16,4,1024]{2,1,0:T(4,128)S(1)}, u32[]{:S(2)}, u32[]{:S(2)}) collective-permute-start(f32[16,4,1024]{2,1,0:T(4,128)} %bitcast.221), channel_id=1, source_target_pairs={{0,1},{1,0},{2,3},{3,2},{4,5},{5,4},{6,7},{7,6},{8,9},{9,8},{10,11... | collective-permute-start | bytes 786440 | tf_op jit(solution)/shard_map/ppermute | solution.py:11
  152.5 20.2 %all-to-all-start.1 = ((f32[16,4,1024]{2,1,0:T(4,128)}), f32[16,4,1024]{2,1,0:T(4,128)S(1)}, u32[]{:S(2)}, u32[]{:S(2)}) async-start(f32[16,4,1024]{2,1,0:T(4,128)} %bitcast_add_fusion.3), calls=%async_computation.1 | async-start | bytes 524288 | tf_op jit(solution)/shard_map/all_to_all | solution.py:105
  162.7 34.7 %copy-start.33 = (s32[8,4]{0,1:T(4,128)S(1)}, s32[8,4]{0,1:T(4,128)}, u32[]{:S(2)}) copy-start(s32[8,4]{0,1:T(4,128)} %copy-done.32) | copy-start | bytes 388
  162.7 34.9 %copy-start.4 = (s32[1,64,8]{2,1,0:T(8,128)S(1)}, s32[1,64,8]{2,1,0:T(8,128)}, u32[]{:S(2)}) copy-start(s32[1,64,8]{2,1,0:T(8,128)} %copy-done.3) | copy-start | bytes 6148
  172.7 18.6 %all-to-all-start.3 = ((f32[16,4,1024]{2,1,0:T(4,128)}), f32[16,4,1024]{2,1,0:T(4,128)S(1)}, u32[]{:S(2)}, u32[]{:S(2)}) async-start(f32[16,4,1024]{2,1,0:T(4,128)} %bitcast_add_fusion.2), calls=%async_computation.3 | async-start | bytes 524288 | tf_op jit(solution)/shard_map/all_to_all | solution.py:105
  179.5 37.1 %copy-start.17 = (s32[8,4,128]{2,0,1:T(8,128)S(1)}, s32[8,4,128]{2,0,1:T(8,128)}, u32[]{:S(2)}) copy-start(s32[8,4,128]{2,0,1:T(8,128)} %copy-done.16) | copy-start | bytes 49156
  179.5 37.1 %copy-start.27 = (s32[512]{0:T(512)S(1)}, s32[512]{0:T(512)}, u32[]{:S(2)}) copy-start(s32[512]{0:T(512)} %copy-done.26) | copy-start | bytes 6148
  179.5 37.1 %copy-start.35 = (s32[8,4]{0,1:T(4,128)S(1)}, s32[8,4]{0,1:T(4,128)}, u32[]{:S(2)}) copy-start(s32[8,4]{0,1:T(4,128)} %copy-done.34) | copy-start | bytes 388
  179.8 37.1 %copy-start.6 = (s32[1,64,8]{2,1,0:T(8,128)S(1)}, s32[1,64,8]{2,1,0:T(8,128)}, u32[]{:S(2)}) copy-start(s32[1,64,8]{2,1,0:T(8,128)} %copy-done.5) | copy-start | bytes 6148
  180.8 19.2 %collective-permute-start.5 = (f32[16,4,1024]{2,1,0:T(4,128)S(1)}, f32[16,4,1024]{2,1,0:T(4,128)S(1)}, u32[]{:S(2)}, u32[]{:S(2)}) collective-permute-start(f32[16,4,1024]{2,1,0:T(4,128)S(1)} %bitcast.264), channel_id=1, source_target_pairs={{0,1},{1,0},{2,3},{3,2},{4,5},{5,4},{6,7},{7,6},{8,9},{9,8},{10,11... | collective-permute-start | bytes 786440 | tf_op jit(solution)/shard_map/ppermute | solution.py:11
  185.9 42.6 %copy-start.23 = (f32[64,64]{1,0:T(8,128)S(1)}, f32[64,64]{1,0:T(8,128)}, u32[]{:S(2)}) copy-start(f32[64,64]{1,0:T(8,128)} %convert_reduce_fusion.3) | copy-start | bytes 49156
  191.3 18.6 %all-to-all-start.7 = ((f32[16,4,1024]{2,1,0:T(4,128)}), f32[16,4,1024]{2,1,0:T(4,128)S(1)}, u32[]{:S(2)}, u32[]{:S(2)}) async-start(f32[16,4,1024]{2,1,0:T(4,128)} %bitcast_add_fusion), calls=%async_computation.7 | async-start | bytes 524288 | tf_op jit(solution)/shard_map/all_to_all | solution.py:105
  209.9 18.2 %all-to-all-start.5 = ((f32[16,4,1024]{2,1,0:T(4,128)}), f32[16,4,1024]{2,1,0:T(4,128)S(1)}, u32[]{:S(2)}, u32[]{:S(2)}) async-start(f32[16,4,1024]{2,1,0:T(4,128)} %bitcast_add_fusion.1), calls=%async_computation.5 | async-start | bytes 524288 | tf_op jit(solution)/shard_map/all_to_all | solution.py:105
  (34 other events, 272.9 us)
Sparse Core Ops, SparseCore 0:
  118.5 127.6 reduce-scatter.3
where the time goes:
time: 258 us; the launch traced here: 256 us
  starting transfers between devices  91.1 us (35%)
  waiting for transfers between devices  84.2 us (33%)
  local copies, waits for them, and re-layouts  32.4 us (13%)
  other arithmetic  21.1 us (8%)
  between operations  15.3 us (6%)
  matrix products  12.2 us (5%)
    all_to_all x4, starting transfers between devices, per_device(): lax.all_to_all(sending.reshape(groups, half_caps, model_width), 'expert',...  35.6 us
    all_to_all x4, waiting for transfers between devices, per_device(): lax.all_to_all(kept_part + partner, 'expert', split_axis=0, concat_axis=0...  34.4 us
    ppermute x8, starting transfers between devices, swapped(): lax.ppermute(x, axis, [(i, i ^ 1 << stride) for i in range(lax.axis_size(...  27.9 us
    all_to_all x4, starting transfers between devices, per_device(): lax.all_to_all(kept_part + partner, 'expert', split_axis=0, concat_axis=0...  27.6 us
    ppermute x8, waiting for transfers between devices, swapped(): lax.ppermute(x, axis, [(i, i ^ 1 << stride) for i in range(lax.axis_size(...  20.5 us
    unnamed x2, waiting for transfers between devices  15.4 us
    all_to_all x4, waiting for transfers between devices, per_device(): lax.all_to_all(sending.reshape(groups, half_caps, model_width), 'expert',...  13.9 us
    unnamed x97, local copies, waits for them, and re-layouts  11.4 us
  transfers between devices with their start and end apart: 17, of which 11 were waited for; matrix products, arithmetic and copies ran while one was open for 16% of the time, Pallas kernels for 0%

commit v1 on v0

v1 whole, which is shorter than its diff:
```python
import jax
import jax.numpy as jnp
from jax import lax
from jax.experimental import pallas as pl
from jax.experimental.pallas import tpu as pltpu
from jax.sharding import PartitionSpec as P

MESH = pl.DeviceIdType.MESH
F32 = jnp.float32
BF16 = jnp.bfloat16

NT = (((1,), (1,)), ((), ()))
TN = (((0,), (0,)), ((), ()))


def kernel(
    dy_hbm, routes_hbm, probs_hbm, disp_hbm, wg_hbm, wu_hbm, wd_hbm,
    gin_ref, gg_ref, gu_ref, gd_ref,
    routes_v, probs_v, dy_v, x_v, wgu, wd, pgu, pd,
    mix_v, s_send, s_recv, act_v, fac_v, hid_v, dg_v, dgp_v, sg_v, ret_v,
    rf, rb, drecv, lsend, lrecv, ssend, srecv, fin, finb, z1, zd,
    in_sem, x_sem, self_sem, ret_self_sem,
    ds_sem, dr_sem, rs_sem, rr_sem,
    ws_sem, wr_sem, sws_sem, swr_sem, cs_sem, cr_sem,
    lss_sem, lsr_sem, sss_sem, ssr_sem, zs_sem, zr_sem,
):
    dp = lax.axis_index("dp")
    mem = lax.axis_index("expert")
    core = dp % 2
    y = (dp // 2) % 8
    zl = dp // 16
    step = 1 - 2 * core
    mine = mem // 2
    zh = mem % 4
    low = (zh * (3 - zh)) // 2

    def peer_of(e):
        return 4 * (e // 2) + low + (e % 2) * (3 - 2 * low)

    partner = mem + 1 - 2 * (mem % 2)
    dp_core = dp + 1 - 2 * core
    dp_fwd = zl * 16 + ((y + step + 8) % 8) * 2 + core
    dp_bwd = zl * 16 + ((y - step + 8) % 8) * 2 + core
    dp_z = (1 - zl) * 16 + y * 2 + core

    def remote(src, dst, ssem, rsem, dev):
        return pltpu.make_async_remote_copy(
            src_ref=src, dst_ref=dst, send_sem=ssem, recv_sem=rsem,
            device_id=dev, device_id_type=MESH,
        )

    barrier = pltpu.get_barrier_semaphore()
    peers = [(dp, peer_of((mine + i) % 8)) for i in range(1, 8)]
    peers += [(dp, partner), (dp_core, mem), (dp_fwd, mem), (dp_bwd, mem), (dp_z, mem), (dp_z, partner)]
    for dev in peers:
        pl.semaphore_signal(barrier, inc=1, device_id=dev, device_id_type=MESH)

    loads = [
        pltpu.make_async_copy(routes_hbm, routes_v, in_sem.at[0]),
        pltpu.make_async_copy(probs_hbm, probs_v, in_sem.at[1]),
        pltpu.make_async_copy(dy_hbm, dy_v, in_sem.at[2]),
        pltpu.make_async_copy(wg_hbm, wgu.at[:, :, :, :, pl.ds(0, 256)], in_sem.at[3]),
        pltpu.make_async_copy(wu_hbm, wgu.at[:, :, :, :, pl.ds(256, 256)], in_sem.at[4]),
        pltpu.make_async_copy(wd_hbm, wd, in_sem.at[5]),
    ]
    for load in loads:
        load.start()
    x_loads = []
    for side in range(2):
        lo = low if side == 0 else 1 - low
        for j in range(8):
            src = 4 * (j // 2) + (lo if j % 2 == 0 else 3 - lo)
            x_loads.append(
                pltpu.make_async_copy(
                    disp_hbm.at[:, pl.ds(pl.multiple_of(src * 8, 8), 8)],
                    x_v.at[side, :, pl.ds(j * 8, 8)],
                    x_sem.at[side, j],
                )
            )
    for load in x_loads:
        load.start()

    for load in loads[:3]:
        load.wait()

    def route(mb, carry):
        ids = routes_v[mb]
        probs = probs_v[mb].astype(F32)
        lane = lax.broadcasted_iota(jnp.int32, (64, 64), 1)
        row = lax.broadcasted_iota(jnp.int32, (64, 64), 0)
        expert = lax.shift_right_logical(lane, 3)
        place = lax.bitwise_and(lane, 7)
        hit = jnp.zeros((64, 64), F32)
        weight = jnp.zeros((64, 64), F32)
        for k in range(8):
            same = ids[:, k : k + 1] == expert
            hit = hit + jnp.where(same, 1.0, 0.0)
            weight = weight + jnp.where(same, probs[:, k : k + 1], 0.0)
        earlier = jnp.where(lane < row, 1.0, 0.0).astype(BF16)
        rank = jnp.dot(earlier, hit.astype(BF16), preferred_element_type=F32)
        chosen = jnp.where(rank == place.astype(F32), hit, 0.0)
        mix_v[mb] = chosen.astype(BF16)
        weighted = (chosen * weight).astype(BF16)
        scaled = lax.dot_general(weighted, dy_v[mb], TN, preferred_element_type=F32)
        s_send[mb] = scaled.astype(BF16)
        return carry

    lax.fori_loop(0, 4, route, 0)
    for load in loads[3:]:
        load.wait()
    pl.semaphore_wait(barrier, len(peers))

    sends = []
    quarter = y % 4

    def weights_copy(n, src_a, src_b, where, side, dev):
        copies = [
            remote(src_a.at[:, where, side], pgu.at[:, where, side], ws_sem.at[n, 0], wr_sem.at[n, 0], dev),
            remote(src_b.at[:, where, side], pd.at[:, where, side], ws_sem.at[n, 1], wr_sem.at[n, 1], dev),
        ]
        return copies

    def start(copies):
        for copy in copies:
            copy.start()
        sends.extend(copies)

    def weights_wait(n, where, side):
        for copy in weights_copy(n, pgu, pd, where, side, (dp_core, mem)):
            copy.wait_recv()

    start(weights_copy(0, wgu, wd, quarter, core, (dp, partner)))

    def slots_copy(src, dst, sem_s, sem_r, chunk, i):
        to = (mine + i) % 8
        return remote(
            src.at[pl.ds(2 * chunk, 2), pl.ds(pl.multiple_of(to * 8, 8), 8)],
            dst.at[pl.ds(2 * chunk, 2), pl.ds(pl.multiple_of(mine * 8, 8), 8)],
            sem_s.at[chunk, i - 1],
            sem_r.at[chunk, i - 1],
            (dp, peer_of(to)),
        )

    def slots_wait(src, dst, sem_s, sem_r, chunk, i):
        came = (mine + 8 - i) % 8
        remote(
            src.at[pl.ds(2 * chunk, 2), pl.ds(pl.multiple_of(came * 8, 8), 8)],
            dst.at[pl.ds(2 * chunk, 2), pl.ds(pl.multiple_of(came * 8, 8), 8)],
            sem_s.at[chunk, i - 1],
            sem_r.at[chunk, i - 1],
            (dp, peer_of((mine + i) % 8)),
        ).wait_recv()

    def slots_self(src, dst, sem, chunk):
        at = pl.ds(pl.multiple_of(mine * 8, 8), 8)
        return pltpu.make_async_copy(
            src.at[pl.ds(2 * chunk, 2), at], dst.at[pl.ds(2 * chunk, 2), at], sem.at[chunk]
        )

    for chunk in range(2):
        start([slots_copy(s_send, s_recv, ds_sem, dr_sem, chunk, i) for i in range(1, 8)])
    for chunk in range(2):
        slots_self(s_send, s_recv, self_sem, chunk).start()

    for load in x_loads:
        load.wait()

    def hidden(half, weights):
        def body(chunk, carry):
            rows = x_v[0, pl.ds(2 * chunk, 2)].reshape(128, 1024)
            both = jnp.dot(rows, weights[...].reshape(1024, 512), preferred_element_type=F32)
            gate, up = both[:, :256], both[:, 256:]
            sig = jax.nn.sigmoid(gate)
            act = gate * sig
            act_v[half, chunk] = act
            fac_v[half, chunk] = up * sig * (1.0 + gate * (1.0 - sig))
            hid_v[chunk, :, pl.ds(256 * half, 256)] = (act * up).astype(BF16)
            return carry

        lax.fori_loop(0, 2, body, 0)

    weights_wait(0, quarter, core)
    start(weights_copy(1, pgu, pd, quarter, core, (dp_fwd, mem)))
    start(weights_copy(2, pgu, pd, quarter, core, (dp_bwd, mem)))
    start(weights_copy(4, pgu, pd, quarter, core, (dp_core, mem)))
    hidden(0, wgu)
    from_bwd = (y - step + 8) % 4
    from_fwd = (y + step + 8) % 4
    across = (y + 2) % 4
    weights_wait(1, from_bwd, core)
    start(weights_copy(3, pgu, pd, from_bwd, core, (dp_fwd, mem)))
    start(weights_copy(5, pgu, pd, from_bwd, core, (dp_core, mem)))
    weights_wait(2, from_fwd, core)
    start(weights_copy(6, pgu, pd, from_fwd, core, (dp_core, mem)))
    weights_wait(3, across, core)
    start(weights_copy(7, pgu, pd, across, core, (dp_core, mem)))
    weights_wait(4, quarter, 1 - core)
    weights_wait(5, from_fwd, 1 - core)
    weights_wait(6, from_bwd, 1 - core)
    weights_wait(7, across, 1 - core)
    hidden(1, pgu)

    def slot_grads(chunk):
        rows = s_recv[pl.ds(2 * chunk, 2)].reshape(128, 1024)
        total = None
        for half, (down, both) in enumerate(((wd, wgu), (pd, pgu))):
            dh = lax.dot_general(rows, down[...].reshape(256, 1024), NT, preferred_element_type=F32)
            d_both = jnp.concatenate(
                [(dh * fac_v[half, chunk]).astype(BF16), (dh * act_v[half, chunk]).astype(BF16)], axis=1
            )
            if half == 0:
                dg_v[0, chunk] = d_both
            else:
                dgp_v[chunk] = d_both
            part = lax.dot_general(d_both, both[...].reshape(1024, 512), NT, preferred_element_type=F32)
            total = part if total is None else total + part
        sg_v[pl.ds(2 * chunk, 2)] = total.astype(BF16).reshape(2, 64, 1024)

    def swap_copy(chunk):
        return remote(
            dgp_v.at[chunk], dg_v.at[1, chunk], sws_sem.at[chunk], swr_sem.at[chunk], (dp, partner)
        )

    for chunk in range(2):
        slots_self(s_send, s_recv, self_sem, chunk).wait()
        for i in range(1, 8):
            slots_wait(s_send, s_recv, ds_sem, dr_sem, chunk, i)
        slot_grads(chunk)
        start([swap_copy(chunk)])
        start([slots_copy(sg_v, ret_v, rs_sem, rr_sem, chunk, i) for i in range(1, 8)])
        slots_self(sg_v, ret_v, ret_self_sem, chunk).start()

    def down_block(q, carry):
        cols = pl.ds(pl.multiple_of(q * 256, 256), 256)
        left = s_recv[:, :, cols].reshape(256, 256)
        out = lax.dot_general(left, hid_v[...].reshape(256, 512), TN, preferred_element_type=F32)
        keep(0, q, out)
        return carry

    def both_block(q, carry):
        cols = pl.ds(pl.multiple_of(q * 256, 256), 256)
        left = x_v[:, :, :, cols].reshape(512, 256)
        out = lax.dot_general(left, dg_v[...].reshape(512, 512), TN, preferred_element_type=F32)
        keep(1, q, out)
        return carry

    def keep(g, q, out):
        out = out.reshape(4, 2, 32, 512)
        at = pl.ds(4 * (q % 2), 4)
        rf[g, q // 2, at] = out
        rb[g, q // 2, at] = out.astype(BF16)

    def core_copy(g):
        return remote(rb.at[g, :, :, 1 - core], drecv.at[g], cs_sem.at[g], cr_sem.at[g], (dp_core, mem))

    def term(g, owner):
        return rf[g, :, owner, core] + drecv[g, :, owner].astype(F32)

    def long_copy(g, t):
        return remote(lsend.at[g, t], lrecv.at[g, t], lss_sem.at[g, t], lsr_sem.at[g, t], (dp_fwd, mem))

    def short_copy(g, t):
        return remote(ssend.at[g, t], srecv.at[g, t], sss_sem.at[g, t], ssr_sem.at[g, t], (dp_bwd, mem))

    def ring_first(g):
        core_copy(g).wait_recv()
        lsend[g, 0] = term(g, (y + 4) % 8).astype(BF16)
        start([long_copy(g, 0)])
        ssend[g, 0] = term(g, (y - 3 * step + 8) % 8).astype(BF16)
        start([short_copy(g, 0)])

    def ring_next(g, t):
        own = term(g, (y + (4 - t) * step + 8) % 8)
        long_copy(g, t - 1).wait_recv()
        lsend[g, t] = (own + lrecv[g, t - 1].astype(F32)).astype(BF16)
        start([long_copy(g, t)])
        if t < 3:
            own = term(g, (y - (3 - t) * step + 8) % 8)
            short_copy(g, t - 1).wait_recv()
            ssend[g, t] = (own + srecv[g, t - 1].astype(F32)).astype(BF16)
            start([short_copy(g, t)])

    def ring_last(g):
        own = term(g, y)
        short_copy(g, 2).wait_recv()
        own = own + srecv[g, 2].astype(F32)
        long_copy(g, 3).wait_recv()
        own = own + lrecv[g, 3].astype(F32)
        fin[g] = own
        finb[g] = own.astype(BF16)

    def z_copies(g):
        if g == 1:
            return [remote(finb.at[1, 1 - zl], z1, zs_sem.at[3], zr_sem.at[3], (dp_z, mem))]
        own, other = pl.ds(0, 256), pl.ds(256, 256)
        return [
            remote(finb.at[0, 1 - zl, :, own], zd.at[0], zs_sem.at[0], zr_sem.at[0], (dp_z, mem)),
            remote(finb.at[0, zl, :, other], zd.at[1], zs_sem.at[1], zr_sem.at[1], (dp, partner)),
            remote(finb.at[0, 1 - zl, :, other], zd.at[2], zs_sem.at[2], zr_sem.at[2], (dp_z, partner)),
        ]

    lax.fori_loop(0, 4, down_block, 0)
    start([core_copy(0)])
    for chunk in range(2):
        swap_copy(chunk).wait_recv()
    ring_first(0)
    lax.fori_loop(0, 4, both_block, 0)
    start([core_copy(1)])

    def tokens(chunk):
        slots_self(sg_v, ret_v, ret_self_sem, chunk).wait()
        for i in range(1, 8):
            slots_wait(sg_v, ret_v, rs_sem, rr_sem, chunk, i)
        for mb in (2 * chunk, 2 * chunk + 1):
            gin_ref[mb] = jnp.dot(mix_v[mb], ret_v[mb], preferred_element_type=F32).astype(BF16)

    ring_first(1)
    ring_next(0, 1)
    ring_next(1, 1)
    tokens(0)
    ring_next(0, 2)
    ring_next(1, 2)
    ring_next(0, 3)
    ring_next(1, 3)
    tokens(1)
    ring_last(0)
    start(z_copies(0))
    ring_last(1)
    start(z_copies(1))

    scale = 1.0 / 128.0
    for copy in z_copies(0):
        copy.wait_recv()
    down = fin[0, zl, :, pl.ds(0, 256)]
    for n in range(3):
        down = down + zd[n].astype(F32)
    gd_ref[...] = down * scale
    for copy in z_copies(1):
        copy.wait_recv()
    both = (fin[1, zl] + z1[...].astype(F32)) * scale
    gg_ref[...] = both[:, :256]
    gu_ref[...] = both[:, 256:]

    for copy in sends:
        copy.wait_send()


def per_device(grad_out, routes, route_probs, dispatched, w_gate, w_up, w_down):
    wg = w_gate.reshape(2, 4, 2, 64, 256)
    wu = w_up.reshape(2, 4, 2, 64, 256)
    wd = w_down.reshape(2, 4, 2, 16, 1024)
    hbm = pl.BlockSpec(memory_space=pl.ANY)
    vmem = pl.BlockSpec(memory_space=pltpu.VMEM)
    dma = pltpu.SemaphoreType.DMA
    V = pltpu.VMEM
    return pl.pallas_call(
        kernel,
        out_shape=(
            jax.ShapeDtypeStruct((4, 64, 1024), BF16),
            jax.ShapeDtypeStruct((32, 256), F32),
            jax.ShapeDtypeStruct((32, 256), F32),
            jax.ShapeDtypeStruct((32, 256), F32),
        ),
        in_specs=[hbm] * 7,
        out_specs=(vmem,) * 4,
        scratch_shapes=[
            V((4, 64, 8), jnp.int32),
            V((4, 64, 8), BF16),
            V((4, 64, 1024), BF16),
            V((2, 4, 64, 1024), BF16),
            V((2, 4, 2, 64, 512), BF16),
            V((2, 4, 2, 16, 1024), BF16),
            V((2, 4, 2, 64, 512), BF16),
            V((2, 4, 2, 16, 1024), BF16),
            V((4, 64, 64), BF16),
            V((4, 64, 1024), BF16),
            V((4, 64, 1024), BF16),
            V((2, 2, 128, 256), F32),
            V((2, 2, 128, 256), F32),
            V((2, 128, 512), BF16),
            V((2, 2, 128, 512), BF16),
            V((2, 128, 512), BF16),
            V((4, 64, 1024), BF16),
            V((4, 64, 1024), BF16),
            V((2, 2, 8, 2, 32, 512), F32),
            V((2, 2, 8, 2, 32, 512), BF16),
            V((2, 2, 8, 32, 512), BF16),
            V((2, 4, 2, 32, 512), BF16),
            V((2, 4, 2, 32, 512), BF16),
            V((2, 3, 2, 32, 512), BF16),
            V((2, 3, 2, 32, 512), BF16),
            V((2, 2, 32, 512), F32),
            V((2, 2, 32, 512), BF16),
            V((32, 512), BF16),
            V((3, 32, 256), BF16),
            dma((6,)), dma((2, 8)), dma((2,)), dma((2,)),
            dma((2, 7)), dma((2, 7)), dma((2, 7)), dma((2, 7)),
            dma((8, 2)), dma((8, 2)), dma((2,)), dma((2,)), dma((2,)), dma((2,)),
            dma((2, 4)), dma((2, 4)), dma((2, 3)), dma((2, 3)), dma((4,)), dma((4,)),
        ],
        compiler_params=pltpu.CompilerParams(
            collective_id=0, has_side_effects=True, vmem_limit_bytes=48 * 1024 * 1024
        ),
        name="moe_backward",
    )(grad_out, routes, route_probs, dispatched, wg, wu, wd)


def solution(mesh):
    return jax.shard_map(
        per_device,
        mesh=mesh,
        in_specs=(
            P(None, ("dp", "expert"), None),
            P(None, ("dp", "expert"), None),
            P(None, ("dp", "expert"), None),
            P(None, ("dp", "expert"), None),
            P(None, "expert"),
            P(None, "expert"),
            P("expert", None),
        ),
        out_specs=(
            P(None, ("dp", "expert"), None),
            P("dp", "expert"),
            P("dp", "expert"),
            P("dp", "expert"),
        ),
        check_vma=False,
    )
```

time: 258 us -> 79.6 us (0.31)
  the two profiles are of different devices: /device:TPU:4 before, /device:TPU:8 now
where the time goes in v1:
time: 79.6 us; the launch traced here: 79.2 us
  Pallas kernels  69.6 us (87%)
  local copies, waits for them, and re-layouts  8.93 us (11%)
    pallas_call x1, Pallas kernels, per_device(): pl.pallas_call(kernel, out_shape=(jax.ShapeDtypeStruct((4, 64, 1024), BF1...  69.6 us
    unnamed x18, local copies, waits for them, and re-layouts  8.93 us

profile of v1, /device:TPU:8, one launch (start us, length us, event | category | flops | bytes accessed | tf_op | source)
XLA Modules:
  0.0 79.2 jit_solution(7275953666309376666)
XLA Ops:
  0.6 0.0 copy-start.5
  0.6 0.8 %copy.12.probs_hbm = bf16[4,64,8]{2,1,0:T(8,128)(2,1)S(1)} copy(bf16[4,64,8]{1,2,0:T(8,128)(2,1)} %param.9) | data formatting | bytes 8192 | tf_op args[2]
  1.5 0.0 copy-done.5
  1.5 0.1 copy.11.routes_hbm
  1.6 0.0 copy-start
  1.6 1.2 %copy-done = bf16[4,128,1024]{2,1,0:T(8,128)(2,1)S(1)} copy-done((bf16[4,128,1024]{2,1,0:T(8,128)(2,1)S(1)}, bf16[4,128,1024]{2,1,0:T(8,128)(2,1)}, u32[]{:S(2)}) %copy-start) | copy-done | bytes 1048600
  2.8 0.0 copy-start.1
  2.8 1.0 %copy-done.1 = bf16[4,64,1024]{2,1,0:T(8,128)(2,1)S(1)} copy-done((bf16[4,64,1024]{2,1,0:T(8,128)(2,1)S(1)}, bf16[4,64,1024]{2,1,0:T(8,128)(2,1)}, u32[]{:S(2)}) %copy-start.1) | copy-done | bytes 524312
  3.8 0.0 copy-start.2
  3.8 1.0 %copy-done.2 = bf16[1024,256]{1,0:T(8,128)(2,1)S(1)} copy-done((bf16[1024,256]{1,0:T(8,128)(2,1)S(1)}, bf16[1024,256]{1,0:T(8,128)(2,1)}, u32[]{:S(2)}) %copy-start.2) | copy-done | bytes 524312
  4.9 0.0 copy-start.3
  4.9 1.0 %copy-done.3 = bf16[1024,256]{1,0:T(8,128)(2,1)S(1)} copy-done((bf16[1024,256]{1,0:T(8,128)(2,1)S(1)}, bf16[1024,256]{1,0:T(8,128)(2,1)}, u32[]{:S(2)}) %copy-start.3) | copy-done | bytes 524312
  5.9 0.0 copy-start.4
  5.9 1.0 %copy-done.4 = bf16[256,1024]{1,0:T(8,128)(2,1)S(1)} copy-done((bf16[256,1024]{1,0:T(8,128)(2,1)S(1)}, bf16[256,1024]{1,0:T(8,128)(2,1)}, u32[]{:S(2)}) %copy-start.4) | copy-done | bytes 524312
  7.0 69.6 %moe_backward.1 = (bf16[4,64,1024]{2,1,0:T(8,128)(2,1)S(1)}, f32[32,256]{1,0:T(8,128)S(1)}, f32[32,256]{1,0:T(8,128)S(1)}, f32[32,256]{1,0:T(8,128)S(1)}) custom-call(bf16[4,64,1024]{2,1,0:T(8,128)(2,1)S(1)} %copy-done.1, s32[4,64,8]{2,1,0:T(8,128)S(1)} %copy.11.routes_hbm, bf16[4,64,8]{2,1,0:T(8,128)(2,1)S(1)} %copy.12.probs_hbm, ...), custom_call_target="tpu_custom_call" | custom-call | tf_op jit(solution)/shard_map/moe_backward/pallas_call | solution.py:356
  76.6 0.8 %copy.17 = bf16[4,64,1024]{2,1,0:T(8,128)(2,1)} copy(bf16[4,64,1024]{2,1,0:T(8,128)(2,1)S(1)} %get-tuple-element.8) | data formatting | bytes 1048576
  77.4 0.6 copy.18
  78.0 0.6 copy.19
  78.6 0.6 copy.20
Async XLA Ops:
  0.6 0.8 %copy-start.5 = (s32[4,64,8]{1,2,0:T(8,128)S(1)}, s32[4,64,8]{1,2,0:T(8,128)}, u32[]{:S(2)}) copy-start(s32[4,64,8]{1,2,0:T(8,128)} %param.8) | copy-start | bytes 24580
  1.6 1.2 %copy-start = (bf16[4,128,1024]{2,1,0:T(8,128)(2,1)S(1)}, bf16[4,128,1024]{2,1,0:T(8,128)(2,1)}, u32[]{:S(2)}) copy-start(bf16[4,128,1024]{2,1,0:T(8,128)(2,1)} %disp_hbm.1) | copy-start | bytes 3145732
  2.8 1.0 %copy-start.1 = (bf16[4,64,1024]{2,1,0:T(8,128)(2,1)S(1)}, bf16[4,64,1024]{2,1,0:T(8,128)(2,1)}, u32[]{:S(2)}) copy-start(bf16[4,64,1024]{2,1,0:T(8,128)(2,1)} %dy_hbm.1) | copy-start | bytes 1572868
  3.8 1.0 %copy-start.2 = (bf16[1024,256]{1,0:T(8,128)(2,1)S(1)}, bf16[1024,256]{1,0:T(8,128)(2,1)}, u32[]{:S(2)}) copy-start(bf16[1024,256]{1,0:T(8,128)(2,1)} %param.11) | copy-start | bytes 1572868
  4.9 1.0 %copy-start.3 = (bf16[1024,256]{1,0:T(8,128)(2,1)S(1)}, bf16[1024,256]{1,0:T(8,128)(2,1)}, u32[]{:S(2)}) copy-start(bf16[1024,256]{1,0:T(8,128)(2,1)} %param.12) | copy-start | bytes 1572868
  5.9 1.0 %copy-start.4 = (bf16[256,1024]{1,0:T(8,128)(2,1)S(1)}, bf16[256,1024]{1,0:T(8,128)(2,1)}, u32[]{:S(2)}) copy-start(bf16[256,1024]{1,0:T(8,128)(2,1)} %param.13) | copy-start | bytes 1572868

commit v2 on v1

v2 whole, which is shorter than its diff:
```python
import jax
import jax.numpy as jnp
from jax import lax
from jax.experimental import pallas as pl
from jax.experimental.pallas import tpu as pltpu
from jax.sharding import PartitionSpec as P

MESH = pl.DeviceIdType.MESH
F32 = jnp.float32
BF16 = jnp.bfloat16

NT = (((1,), (1,)), ((), ()))
TN = (((0,), (0,)), ((), ()))


def kernel(
    dy_hbm, routes_hbm, probs_hbm, disp_hbm, wg_hbm, wu_hbm, wd_hbm,
    gin_hbm, gg_hbm, gu_hbm, gd_hbm,
    routes_v, probs_v, dy_v, x_v, wgu, wd, pgu, pd,
    mix_v, s_send, s_recv, act_v, fac_v, hid_v, dg_v, sg_v, ret_v,
    rf, rb, drecv, lsend, lrecv, ssend, srecv, fin, finb, zd, gin_v, gate_v, up_v, down_v,
    in_sem, x_sem, out_sem, self_sem, ret_self_sem,
    ds_sem, dr_sem, rs_sem, rr_sem,
    ws_sem, wr_sem, cs_sem, cr_sem,
    lss_sem, lsr_sem, sss_sem, ssr_sem, zs_sem, zr_sem,
):
    dp = lax.axis_index("dp")
    mem = lax.axis_index("expert")
    core = dp % 2
    y = (dp // 2) % 8
    zl = dp // 16
    step = 1 - 2 * core
    mine = mem // 2
    zh = mem % 4
    low = (zh * (3 - zh)) // 2

    def peer_of(e):
        return 4 * (e // 2) + low + (e % 2) * (3 - 2 * low)

    partner = mem + 1 - 2 * (mem % 2)
    dp_core = dp + 1 - 2 * core
    dp_fwd = zl * 16 + ((y + step + 8) % 8) * 2 + core
    dp_bwd = zl * 16 + ((y - step + 8) % 8) * 2 + core
    dp_z = (1 - zl) * 16 + y * 2 + core

    def remote(src, dst, ssem, rsem, dev):
        return pltpu.make_async_remote_copy(
            src_ref=src, dst_ref=dst, send_sem=ssem, recv_sem=rsem,
            device_id=dev, device_id_type=MESH,
        )

    barrier = pltpu.get_barrier_semaphore()
    peers = [(dp, peer_of((mine + i) % 8)) for i in range(1, 8)]
    peers += [(dp, partner), (dp_core, mem), (dp_fwd, mem), (dp_bwd, mem), (dp_z, mem), (dp_z, partner)]
    for dev in peers:
        pl.semaphore_signal(barrier, inc=1, device_id=dev, device_id_type=MESH)

    loads = [
        pltpu.make_async_copy(wg_hbm, wgu.at[:, :, :, :, pl.ds(0, 256)], in_sem.at[3]),
        pltpu.make_async_copy(wu_hbm, wgu.at[:, :, :, :, pl.ds(256, 256)], in_sem.at[4]),
        pltpu.make_async_copy(wd_hbm, wd, in_sem.at[5]),
        pltpu.make_async_copy(routes_hbm, routes_v, in_sem.at[0]),
        pltpu.make_async_copy(probs_hbm, probs_v, in_sem.at[1]),
        pltpu.make_async_copy(dy_hbm, dy_v, in_sem.at[2]),
    ]
    for load in loads:
        load.start()
    with jax.named_scope("barrier"):
        for load in loads[:3]:
            load.wait()
        pl.semaphore_wait(barrier, len(peers))

    sends = []
    quarter = y % 4

    def weights_copy(n, h, src_a, src_b, where, side, dev, come=None):
        come = n if come is None else come
        return [
            remote(
                src_a.at[h, where, side], pgu.at[h, where, side], ws_sem.at[n, h, 0], wr_sem.at[come, h, 0], dev
            ),
            remote(
                src_b.at[h, where, side], pd.at[h, where, side], ws_sem.at[n, h, 1], wr_sem.at[come, h, 1], dev
            ),
        ]

    def start(copies):
        for copy in copies:
            copy.start()
        sends.extend(copies)

    def weights_wait(n, h, where, side):
        for copy in weights_copy(n, h, pgu, pd, where, side, (dp_core, mem)):
            copy.wait_recv()

    def pass_on(n, h, where, dev):
        start(weights_copy(n, h, pgu, pd, where, core, dev))

    near = (zl + zh) % 2 == 1
    far = (zl + zh) % 2 == 0
    near_sends = []
    for h in range(2):
        near_sends += weights_copy(0, h, wgu, wd, quarter, core, (dp_z, partner))

    @pl.when(near)
    def _():
        for copy in near_sends:
            copy.start()

    with jax.named_scope("wait_in"):
        for load in loads[3:]:
            load.wait()

    def route(mb, carry):
        ids = routes_v[mb]
        probs = probs_v[mb].astype(F32)
        lane = lax.broadcasted_iota(jnp.int32, (64, 64), 1)
        row = lax.broadcasted_iota(jnp.int32, (64, 64), 0)
        expert = lax.shift_right_logical(row, 3)
        place = lax.bitwise_and(row, 7)
        hit = jnp.zeros((64, 64), F32)
        weight = jnp.zeros((64, 64), F32)
        for k in range(8):
            same = ids[k : k + 1, :] == expert
            hit = hit + jnp.where(same, 1.0, 0.0)
            weight = weight + jnp.where(same, probs[k : k + 1, :], 0.0)
        earlier = jnp.where(row < lane, 1.0, 0.0).astype(BF16)
        rank = jnp.dot(hit.astype(BF16), earlier, preferred_element_type=F32)
        chosen = jnp.where(rank == place.astype(F32), hit, 0.0)
        mix_v[mb] = chosen.astype(BF16)
        weighted = (chosen * weight).astype(BF16)
        scaled = jnp.dot(weighted, dy_v[mb], preferred_element_type=F32)
        s_send[mb] = scaled.astype(BF16)
        return carry

    x_loads = []
    for j in range(8):
        src = 4 * (j // 2) + (low if j % 2 == 0 else 3 - low)
        x_loads.append(
            pltpu.make_async_copy(
                disp_hbm.at[:, pl.ds(pl.multiple_of(src * 8, 8), 8)],
                x_v.at[:, pl.ds(j * 8, 8)],
                x_sem.at[j],
            )
        )
    for load in x_loads:
        load.start()
    with jax.named_scope("route"):
        lax.fori_loop(0, 4, route, 0)
    def slots_copy(src, dst, sem_s, sem_r, chunk, i):
        to = (mine + i) % 8
        return remote(
            src.at[pl.ds(2 * chunk, 2), pl.ds(pl.multiple_of(to * 8, 8), 8)],
            dst.at[pl.ds(2 * chunk, 2), pl.ds(pl.multiple_of(mine * 8, 8), 8)],
            sem_s.at[chunk, i - 1],
            sem_r.at[chunk, i - 1],
            (dp, peer_of(to)),
        )

    def slots_wait(src, dst, sem_s, sem_r, chunk, i):
        came = (mine + 8 - i) % 8
        remote(
            src.at[pl.ds(2 * chunk, 2), pl.ds(pl.multiple_of(came * 8, 8), 8)],
            dst.at[pl.ds(2 * chunk, 2), pl.ds(pl.multiple_of(came * 8, 8), 8)],
            sem_s.at[chunk, i - 1],
            sem_r.at[chunk, i - 1],
            (dp, peer_of((mine + i) % 8)),
        ).wait_recv()

    def slots_self(src, dst, sem, chunk):
        at = pl.ds(pl.multiple_of(mine * 8, 8), 8)
        return pltpu.make_async_copy(
            src.at[pl.ds(2 * chunk, 2), at], dst.at[pl.ds(2 * chunk, 2), at], sem.at[chunk]
        )

    crossing = [slots_copy(s_send, s_recv, ds_sem, dr_sem, chunk, i) for chunk in range(2) for i in (1, 3, 5, 7)]
    for chunk in range(2):
        start([slots_copy(s_send, s_recv, ds_sem, dr_sem, chunk, i) for i in (2, 4, 6)])
        slots_self(s_send, s_recv, self_sem, chunk).start()
    sends.extend(crossing)

    @pl.when(far)
    def _():
        for copy in crossing:
            copy.start()

    with jax.named_scope("wait_x"):
        for load in x_loads:
            load.wait()

    def hidden(half, weights):
        def body(chunk, carry):
            rows = x_v[pl.ds(2 * chunk, 2)].reshape(128, 1024)
            both = jnp.dot(rows, weights[...].reshape(1024, 512), preferred_element_type=F32)
            gate, up = both[:, :256], both[:, 256:]
            sig = jax.nn.sigmoid(gate)
            act = gate * sig
            act_v[half, chunk] = act
            fac_v[half, chunk] = up * sig * (1.0 + gate * (1.0 - sig))
            hid_v[chunk, :, pl.ds(256 * half, 256)] = (act * up).astype(BF16)
            return carry

        lax.fori_loop(0, 2, body, 0)

    def d_terms(half, chunk, down):
        rows = s_recv[pl.ds(2 * chunk, 2)].reshape(128, 1024)
        dh = lax.dot_general(rows, down[...].reshape(256, 1024), NT, preferred_element_type=F32)
        d_both = jnp.concatenate(
            [(dh * fac_v[half, chunk]).astype(BF16), (dh * act_v[half, chunk]).astype(BF16)], axis=1
        )
        dg_v[half, chunk] = d_both

    def slot_grads(chunk):
        total = lax.dot_general(
            dg_v[0, chunk], wgu[...].reshape(1024, 512), NT, preferred_element_type=F32
        ) + lax.dot_general(dg_v[1, chunk], pgu[...].reshape(1024, 512), NT, preferred_element_type=F32)
        sg_v[pl.ds(2 * chunk, 2)] = total.astype(BF16).reshape(2, 64, 1024)

    def weight_terms(half, s):
        z = (zl + 1 + s) % 2

        def body(q, carry):
            cols = pl.ds(pl.multiple_of((2 * z + q) * 256, 256), 256)
            at = pl.ds(4 * q, 4)
            right = hid_v[:, :, pl.ds(256 * half, 256)].reshape(256, 256)
            out = lax.dot_general(s_recv[:, :, cols].reshape(256, 256), right, TN, preferred_element_type=F32)
            out = out.reshape(4, 2, 32, 256)
            rf[half, s, at, :, :, pl.ds(0, 256)] = out
            rb[half, s, at, :, :, pl.ds(0, 256)] = out.astype(BF16)
            right = dg_v[half].reshape(256, 512)
            out = lax.dot_general(x_v[:, :, cols].reshape(256, 256), right, TN, preferred_element_type=F32)
            out = out.reshape(4, 2, 32, 512)
            rf[half, s, at, :, :, pl.ds(256, 512)] = out
            rb[half, s, at, :, :, pl.ds(256, 512)] = out.astype(BF16)
            return carry

        lax.fori_loop(0, 2, body, 0)
        start([core_copy(half, s)])

    def core_copy(g, s):
        return remote(rb.at[g, s, :, 1 - core], drecv.at[g, s], cs_sem.at[g, s], cr_sem.at[g, s], (dp_core, mem))

    def term(g, s, owner):
        return rf[g, s, owner, core] + drecv[g, s, owner].astype(F32)

    def long_copy(g, s, t):
        at = (g, s, t)
        return remote(lsend.at[at], lrecv.at[at], lss_sem.at[at], lsr_sem.at[at], (dp_fwd, mem))

    def short_copy(g, s, t):
        at = (g, s, t)
        return remote(ssend.at[at], srecv.at[at], sss_sem.at[at], ssr_sem.at[at], (dp_bwd, mem))

    def ring_first(g, s):
        core_copy(g, s).wait_recv()
        lsend[g, s, 0] = term(g, s, (y + 4) % 8).astype(BF16)
        start([long_copy(g, s, 0)])
        ssend[g, s, 0] = term(g, s, (y - 3 * step + 8) % 8).astype(BF16)
        start([short_copy(g, s, 0)])

    def ring_next(g, s, t):
        own = term(g, s, (y + (4 - t) * step + 8) % 8)
        long_copy(g, s, t - 1).wait_recv()
        lsend[g, s, t] = (own + lrecv[g, s, t - 1].astype(F32)).astype(BF16)
        start([long_copy(g, s, t)])
        if t < 3:
            own = term(g, s, (y - (3 - t) * step + 8) % 8)
            short_copy(g, s, t - 1).wait_recv()
            ssend[g, s, t] = (own + srecv[g, s, t - 1].astype(F32)).astype(BF16)
            start([short_copy(g, s, t)])

    def z_copy(g, s):
        n = (0, None, 1, 2)[2 * g + s]
        dev = ((dp_z, dp)[s], (mem, partner)[g])
        return remote(finb.at[g, s], zd.at[n], zs_sem.at[n], zr_sem.at[n], dev)

    def ring_last(g, s):
        own = term(g, s, y)
        short_copy(g, s, 2).wait_recv()
        own = own + srecv[g, s, 2].astype(F32)
        long_copy(g, s, 3).wait_recv()
        own = own + lrecv[g, s, 3].astype(F32)
        if g == 0 and s == 1:
            fin[...] = own
        else:
            finb[g, s] = own.astype(BF16)
            start([z_copy(g, s)])

    def slots_arrive(chunk):
        slots_self(s_send, s_recv, self_sem, chunk).wait()
        for i in range(1, 8):
            slots_wait(s_send, s_recv, ds_sem, dr_sem, chunk, i)

    from_bwd = (y - step + 8) % 4
    from_fwd = (y + step + 8) % 4
    across = (y + 2) % 4

    def first_piece(h):
        weights_wait(0, h, quarter, core)
        relays = weights_copy(8, h, pgu, pd, quarter, core, (dp_z, mem), 0)
        near_sends.extend(relays)

        @pl.when(near)
        def _():
            for copy in relays:
                copy.start()

        pass_on(1, h, quarter, (dp_fwd, mem))
        pass_on(2, h, quarter, (dp_bwd, mem))
        pass_on(4, h, quarter, (dp_core, mem))

    def second_piece(h):
        weights_wait(1, h, from_bwd, core)
        pass_on(3, h, from_bwd, (dp_fwd, mem))
        pass_on(5, h, from_bwd, (dp_core, mem))
        weights_wait(2, h, from_fwd, core)
        pass_on(6, h, from_fwd, (dp_core, mem))

    def third_piece(h):
        weights_wait(3, h, across, core)
        pass_on(7, h, across, (dp_core, mem))

    def last_piece(h):
        weights_wait(4, h, quarter, 1 - core)
        weights_wait(5, h, from_fwd, 1 - core)
        weights_wait(6, h, from_bwd, 1 - core)
        weights_wait(7, h, across, 1 - core)

    stores = []

    def store(src, dst, n):
        copy = pltpu.make_async_copy(src, dst, out_sem.at[n])
        copy.start()
        stores.append(copy)

    def tokens(chunk):
        slots_self(sg_v, ret_v, ret_self_sem, chunk).wait()
        for i in range(1, 8):
            slots_wait(sg_v, ret_v, rs_sem, rr_sem, chunk, i)
        for mb in (2 * chunk, 2 * chunk + 1):
            gin_v[mb] = lax.dot_general(mix_v[mb], ret_v[mb], TN, preferred_element_type=F32).astype(BF16)
        half = pl.ds(2 * chunk, 2)
        store(gin_v.at[half], gin_hbm.at[half], chunk)

    with jax.named_scope("hidden0"):
        hidden(0, wgu)
    with jax.named_scope("w0a"):
        first_piece(0)
    with jax.named_scope("w0b"):
        first_piece(1)

    @pl.when(near)
    def _():
        for copy in crossing:
            copy.start()

    with jax.named_scope("w1a"):
        second_piece(0)
    with jax.named_scope("w1b"):
        second_piece(1)
    with jax.named_scope("w3a"):
        third_piece(0)
    with jax.named_scope("slots0"):
        slots_arrive(0)
    with jax.named_scope("d_own0"):
        d_terms(0, 0, wd)
    with jax.named_scope("w3b"):
        third_piece(1)
    with jax.named_scope("slots1"):
        slots_arrive(1)
    with jax.named_scope("d_own1"):
        d_terms(0, 1, wd)
    with jax.named_scope("weights0"):
        weight_terms(0, 0)
        weight_terms(0, 1)
    with jax.named_scope("ring_first0"):
        ring_first(0, 0)
        ring_first(0, 1)
    with jax.named_scope("wlast"):
        last_piece(0)
        last_piece(1)
    with jax.named_scope("hidden1"):
        hidden(1, pgu)
    with jax.named_scope("d_partner"):
        d_terms(1, 0, pd)
        d_terms(1, 1, pd)
    with jax.named_scope("ring_next0_1a"):
        ring_next(0, 0, 1)
    with jax.named_scope("slot_grads0"):
        slot_grads(0)
        start([slots_copy(sg_v, ret_v, rs_sem, rr_sem, 0, i) for i in range(1, 8)])
        slots_self(sg_v, ret_v, ret_self_sem, 0).start()
    with jax.named_scope("weights1"):
        weight_terms(1, 0)
        weight_terms(1, 1)
    with jax.named_scope("ring_next0_1b"):
        ring_next(0, 1, 1)
    with jax.named_scope("slot_grads1"):
        slot_grads(1)
        start([slots_copy(sg_v, ret_v, rs_sem, rr_sem, 1, i) for i in range(1, 8)])
        slots_self(sg_v, ret_v, ret_self_sem, 1).start()
    with jax.named_scope("ring_first1"):
        ring_first(1, 0)
        ring_first(1, 1)
    with jax.named_scope("ring_next0_2"):
        ring_next(0, 0, 2)
        ring_next(0, 1, 2)
    with jax.named_scope("ring_next1_1"):
        ring_next(1, 0, 1)
        ring_next(1, 1, 1)
    with jax.named_scope("ring_next0_3"):
        ring_next(0, 0, 3)
        ring_next(0, 1, 3)
    with jax.named_scope("ring_next1_2"):
        ring_next(1, 0, 2)
        ring_next(1, 1, 2)
    with jax.named_scope("ring_last0"):
        ring_last(0, 0)
        ring_last(0, 1)
    with jax.named_scope("tokens0"):
        tokens(0)
    with jax.named_scope("ring_next1_3"):
        ring_next(1, 0, 3)
        ring_next(1, 1, 3)
    with jax.named_scope("tokens1"):
        tokens(1)
    with jax.named_scope("ring_last1"):
        ring_last(1, 0)
        ring_last(1, 1)

    with jax.named_scope("wait_z"):
        for copy in (z_copy(0, 0), z_copy(1, 0), z_copy(1, 1)):
            copy.wait_recv()
    total = fin[...]
    for n in range(3):
        total = total + zd[n].astype(F32)
    total = total * (1.0 / 128.0)
    down_v[...] = total[:, :256]
    store(down_v, gd_hbm, 2)
    gate_v[...] = total[:, 256:512]
    store(gate_v, gg_hbm, 3)
    up_v[...] = total[:, 512:]
    store(up_v, gu_hbm, 4)

    with jax.named_scope("wait_sends"):
        for copy in sends:
            copy.wait_send()
        for copy in stores:
            copy.wait()

        @pl.when(near)
        def _():
            for copy in near_sends:
                copy.wait_send()


def per_device(grad_out, routes, route_probs, dispatched, w_gate, w_up, w_down):
    wg = w_gate.reshape(2, 4, 2, 64, 256)
    wu = w_up.reshape(2, 4, 2, 64, 256)
    wd = w_down.reshape(2, 4, 2, 16, 1024)
    hbm = pl.BlockSpec(memory_space=pltpu.HBM)
    vmem = pl.BlockSpec(memory_space=pltpu.VMEM)
    dma = pltpu.SemaphoreType.DMA
    V = pltpu.VMEM
    results = pl.pallas_call(
        kernel,
        out_shape=(
            jax.ShapeDtypeStruct((4, 64, 1024), BF16),
            jax.ShapeDtypeStruct((32, 256), F32),
            jax.ShapeDtypeStruct((32, 256), F32),
            jax.ShapeDtypeStruct((32, 256), F32),
        ),
        in_specs=[hbm] * 7,
        out_specs=(hbm,) * 4,
        scratch_shapes=[
            V((4, 8, 64), jnp.int32),
            V((4, 8, 64), BF16),
            V((4, 64, 1024), BF16),
            V((4, 64, 1024), BF16),
            V((2, 4, 2, 64, 512), BF16),
            V((2, 4, 2, 16, 1024), BF16),
            V((2, 4, 2, 64, 512), BF16),
            V((2, 4, 2, 16, 1024), BF16),
            V((4, 64, 64), BF16),
            V((4, 64, 1024), BF16),
            V((4, 64, 1024), BF16),
            V((2, 2, 128, 256), F32),
            V((2, 2, 128, 256), F32),
            V((2, 128, 512), BF16),
            V((2, 2, 128, 512), BF16),
            V((4, 64, 1024), BF16),
            V((4, 64, 1024), BF16),
            V((2, 2, 8, 2, 32, 768), F32),
            V((2, 2, 8, 2, 32, 768), BF16),
            V((2, 2, 8, 32, 768), BF16),
            V((2, 2, 4, 32, 768), BF16),
            V((2, 2, 4, 32, 768), BF16),
            V((2, 2, 3, 32, 768), BF16),
            V((2, 2, 3, 32, 768), BF16),
            V((32, 768), F32),
            V((2, 2, 32, 768), BF16),
            V((3, 32, 768), BF16),
            V((4, 64, 1024), BF16),
            V((32, 256), F32),
            V((32, 256), F32),
            V((32, 256), F32),
            dma((6,)), dma((8,)), dma((5,)), dma((2,)), dma((2,)),
            dma((2, 7)), dma((2, 7)), dma((2, 7)), dma((2, 7)),
            dma((9, 2, 2)), dma((8, 2, 2)), dma((2, 2)), dma((2, 2)),
            dma((2, 2, 4)), dma((2, 2, 4)), dma((2, 2, 3)), dma((2, 2, 3)), dma((3,)), dma((3,)),
        ],
        compiler_params=pltpu.CompilerParams(
            collective_id=0, has_side_effects=True, vmem_limit_bytes=62000000
        ),
        name="moe_backward",
    )(grad_out, jnp.swapaxes(routes, 1, 2), jnp.swapaxes(route_probs, 1, 2), dispatched, wg, wu, wd)

    def store(a, b, c, d, out_a, out_b, out_c, out_d, sem):
        copies = [
            pltpu.make_async_copy(src, dst, sem.at[n])
            for n, (src, dst) in enumerate(((a, out_a), (b, out_b), (c, out_c), (d, out_d)))
        ]
        for copy in copies:
            copy.start()
        for copy in copies:
            copy.wait()

    return pl.pallas_call(
        store,
        out_shape=tuple(jax.ShapeDtypeStruct(r.shape, r.dtype) for r in results),
        in_specs=[vmem] * 4,
        out_specs=(hbm,) * 4,
        scratch_shapes=[dma((4,))],
        name="store_results",
    )(*results)


def solution(mesh):
    return jax.shard_map(
        per_device,
        mesh=mesh,
        in_specs=(
            P(None, ("dp", "expert"), None),
            P(None, ("dp", "expert"), None),
            P(None, ("dp", "expert"), None),
            P(None, ("dp", "expert"), None),
            P(None, "expert"),
            P(None, "expert"),
            P("expert", None),
        ),
        out_specs=(
            P(None, ("dp", "expert"), None),
            P("dp", "expert"),
            P("dp", "expert"),
            P("dp", "expert"),
        ),
        check_vma=False,
    )
```

time: 79.6 us -> 66.8 us (0.84)
  local copies, waits for them, and re-layouts: 8.93 us -> 0 us
  Pallas kernels: 69.6 us -> 66 us
    unnamed x18 -> x0, local copies, waits for them, and re-layouts: 8.93 us -> none
    pallas_call x1, Pallas kernels: 69.6 us -> 64.1 us  [per_device(): pl.pallas_call(kernel, out_shape=(jax.ShapeDtypeStruct((4, 64, 1024), BF1...]
    pallas_call x0 -> x1, Pallas kernels: none -> 1.91 us  [per_device(): pl.pallas_call(store, out_shape=tuple((jax.ShapeDtypeStruct(r.shape, r.dt...]
where the time goes in v2:
time: 66.8 us; the launch traced here: 66.6 us
  Pallas kernels  66 us (99%)
    pallas_call x1, Pallas kernels, per_device(): pl.pallas_call(kernel, out_shape=(jax.ShapeDtypeStruct((4, 64, 1024), BF1...  64.1 us
    pallas_call x1, Pallas kernels, per_device(): pl.pallas_call(store, out_shape=tuple((jax.ShapeDtypeStruct(r.shape, r.dt...  1.91 us

profile of v2, /device:TPU:8, one launch (start us, length us, event | category | flops | bytes accessed | tf_op | source)
XLA Modules:
  0.0 66.6 jit_solution(2344751214918836978)
XLA Ops:
  0.6 64.1 %moe_backward.1 = (bf16[4,64,1024]{2,1,0:T(8,128)(2,1)}, f32[32,256]{1,0:T(8,128)}, f32[32,256]{1,0:T(8,128)}, f32[32,256]{1,0:T(8,128)}) custom-call(bf16[4,64,1024]{2,1,0:T(8,128)(2,1)} %dy_hbm.1, s32[4,8,64]{2,1,0:T(8,128)} %bitcast.8, bf16[4,8,64]{2,1,0:T(8,128)(2,1)} %bitcast.9, bf16[4,128,1024]{2,1,0:T(8,128)(2,1)} %disp_hbm.1, ...), custom_call_target="tpu_custom_call" | custom-call | tf_op jit(solution)/shard_map/moe_backward/pallas_call | solution.py:465
  64.7 1.9 %store_results.1 = (bf16[4,64,1024]{2,1,0:T(8,128)(2,1)}, f32[32,256]{1,0:T(8,128)}, f32[32,256]{1,0:T(8,128)}, f32[32,256]{1,0:T(8,128)}) custom-call(bf16[4,64,1024]{2,1,0:T(8,128)(2,1)} %get-tuple-element.8.a, f32[32,256]{1,0:T(8,128)} %get-tuple-element.9.b, f32[32,256]{1,0:T(8,128)} %get-tuple-element.10.c, f32[32,256]{1,0:T(8,128)} %get-tuple-element.11.d), custom_call_target="tpu_custom_call" | custom-call | tf_op jit(solution)/shard_map/store_results/pallas_call | solution.py:528

commit v3 on v2

--- a/solution.py
+++ b/solution.py
@@ -15,14 +15,14 @@
 
 def kernel(
     dy_hbm, routes_hbm, probs_hbm, disp_hbm, wg_hbm, wu_hbm, wd_hbm,
-    gin_hbm, gg_hbm, gu_hbm, gd_hbm,
+    gin_v, gate_v, up_v, down_v,
     routes_v, probs_v, dy_v, x_v, wgu, wd, pgu, pd,
     mix_v, s_send, s_recv, act_v, fac_v, hid_v, dg_v, sg_v, ret_v,
-    rf, rb, drecv, lsend, lrecv, ssend, srecv, fin, finb, zd, gin_v, gate_v, up_v, down_v,
-    in_sem, x_sem, out_sem, self_sem, ret_self_sem,
+    rf, rb, drecv, lsend, lrecv, ssend, srecv, fin, finb, zd,
+    in_sem, x_sem,
     ds_sem, dr_sem, rs_sem, rr_sem,
     ws_sem, wr_sem, cs_sem, cr_sem,
-    lss_sem, lsr_sem, sss_sem, ssr_sem, zs_sem, zr_sem,
+    lsr_sem, ssr_sem, zr_sem,
 ):
     dp = lax.axis_index("dp")
     mem = lax.axis_index("expert")
@@ -70,24 +70,19 @@
             load.wait()
         pl.semaphore_wait(barrier, len(peers))
 
-    sends = []
     quarter = y % 4
 
     def weights_copy(n, h, src_a, src_b, where, side, dev, come=None):
         come = n if come is None else come
+        kind = 0 if 0 < n < 8 else 1
         return [
-            remote(
-                src_a.at[h, where, side], pgu.at[h, where, side], ws_sem.at[n, h, 0], wr_sem.at[come, h, 0], dev
-            ),
-            remote(
-                src_b.at[h, where, side], pd.at[h, where, side], ws_sem.at[n, h, 1], wr_sem.at[come, h, 1], dev
-            ),
+            remote(src_a.at[h, where, side], pgu.at[h, where, side], ws_sem.at[kind, 0], wr_sem.at[come, h, 0], dev),
+            remote(src_b.at[h, where, side], pd.at[h, where, side], ws_sem.at[kind, 1], wr_sem.at[come, h, 1], dev),
         ]
 
     def start(copies):
         for copy in copies:
             copy.start()
-        sends.extend(copies)
 
     def weights_wait(n, h, where, side):
         for copy in weights_copy(n, h, pgu, pd, where, side, (dp_core, mem)):
@@ -140,53 +135,47 @@
             pltpu.make_async_copy(
                 disp_hbm.at[:, pl.ds(pl.multiple_of(src * 8, 8), 8)],
                 x_v.at[:, pl.ds(j * 8, 8)],
-                x_sem.at[j],
+                x_sem.at[0],
             )
         )
     for load in x_loads:
         load.start()
-    with jax.named_scope("route"):
-        lax.fori_loop(0, 4, route, 0)
     def slots_copy(src, dst, sem_s, sem_r, chunk, i):
         to = (mine + i) % 8
         return remote(
             src.at[pl.ds(2 * chunk, 2), pl.ds(pl.multiple_of(to * 8, 8), 8)],
             dst.at[pl.ds(2 * chunk, 2), pl.ds(pl.multiple_of(mine * 8, 8), 8)],
-            sem_s.at[chunk, i - 1],
-            sem_r.at[chunk, i - 1],
+            sem_s.at[0],
+            sem_r.at[chunk],
             (dp, peer_of(to)),
         )
 
-    def slots_wait(src, dst, sem_s, sem_r, chunk, i):
-        came = (mine + 8 - i) % 8
-        remote(
-            src.at[pl.ds(2 * chunk, 2), pl.ds(pl.multiple_of(came * 8, 8), 8)],
-            dst.at[pl.ds(2 * chunk, 2), pl.ds(pl.multiple_of(came * 8, 8), 8)],
-            sem_s.at[chunk, i - 1],
-            sem_r.at[chunk, i - 1],
-            (dp, peer_of((mine + i) % 8)),
-        ).wait_recv()
-
-    def slots_self(src, dst, sem, chunk):
+    def slots_self(src, dst, sem_r, chunk):
         at = pl.ds(pl.multiple_of(mine * 8, 8), 8)
         return pltpu.make_async_copy(
-            src.at[pl.ds(2 * chunk, 2), at], dst.at[pl.ds(2 * chunk, 2), at], sem.at[chunk]
+            src.at[pl.ds(2 * chunk, 2), at], dst.at[pl.ds(2 * chunk, 2), at], sem_r.at[chunk]
         )
 
-    crossing = [slots_copy(s_send, s_recv, ds_sem, dr_sem, chunk, i) for chunk in range(2) for i in (1, 3, 5, 7)]
+    def slots_wait(dst, sem_r, chunk):
+        rows = dst.at[pl.ds(2 * chunk, 2)]
+        pltpu.make_async_copy(rows, rows, sem_r.at[chunk]).wait()
+
+    crossing = []
     for chunk in range(2):
+        with jax.named_scope("route"):
+            lax.fori_loop(2 * chunk, 2 * chunk + 2, route, 0)
         start([slots_copy(s_send, s_recv, ds_sem, dr_sem, chunk, i) for i in (2, 4, 6)])
-        slots_self(s_send, s_recv, self_sem, chunk).start()
-    sends.extend(crossing)
-
-    @pl.when(far)
-    def _():
-        for copy in crossing:
-            copy.start()
+        slots_self(s_send, s_recv, dr_sem, chunk).start()
+        across_z = [slots_copy(s_send, s_recv, ds_sem, dr_sem, chunk, i) for i in (1, 3, 5, 7)]
+        crossing.extend(across_z)
+
+        @pl.when(far)
+        def _():
+            for copy in across_z:
+                copy.start()
 
     with jax.named_scope("wait_x"):
-        for load in x_loads:
-            load.wait()
+        pltpu.make_async_copy(x_v, x_v, x_sem.at[0]).wait()
 
     def hidden(half, weights):
         def body(chunk, carry):
@@ -238,18 +227,18 @@
         start([core_copy(half, s)])
 
     def core_copy(g, s):
-        return remote(rb.at[g, s, :, 1 - core], drecv.at[g, s], cs_sem.at[g, s], cr_sem.at[g, s], (dp_core, mem))
+        return remote(rb.at[g, s, :, 1 - core], drecv.at[g, s], cs_sem.at[0], cr_sem.at[g, s], (dp_core, mem))
 
     def term(g, s, owner):
         return rf[g, s, owner, core] + drecv[g, s, owner].astype(F32)
 
     def long_copy(g, s, t):
         at = (g, s, t)
-        return remote(lsend.at[at], lrecv.at[at], lss_sem.at[at], lsr_sem.at[at], (dp_fwd, mem))
+        return remote(lsend.at[at], lrecv.at[at], cs_sem.at[1], lsr_sem.at[at], (dp_fwd, mem))
 
     def short_copy(g, s, t):
         at = (g, s, t)
-        return remote(ssend.at[at], srecv.at[at], sss_sem.at[at], ssr_sem.at[at], (dp_bwd, mem))
+        return remote(ssend.at[at], srecv.at[at], cs_sem.at[2], ssr_sem.at[at], (dp_bwd, mem))
 
     def ring_first(g, s):
         core_copy(g, s).wait_recv()
@@ -272,7 +261,7 @@
     def z_copy(g, s):
         n = (0, None, 1, 2)[2 * g + s]
         dev = ((dp_z, dp)[s], (mem, partner)[g])
-        return remote(finb.at[g, s], zd.at[n], zs_sem.at[n], zr_sem.at[n], dev)
+        return remote(finb.at[g, s], zd.at[n], cs_sem.at[3], zr_sem.at[n], dev)
 
     def ring_last(g, s):
         own = term(g, s, y)
@@ -287,9 +276,7 @@
             start([z_copy(g, s)])
 
     def slots_arrive(chunk):
-        slots_self(s_send, s_recv, self_sem, chunk).wait()
-        for i in range(1, 8):
-            slots_wait(s_send, s_recv, ds_sem, dr_sem, chunk, i)
+        slots_wait(s_recv, dr_sem, chunk)
 
     from_bwd = (y - step + 8) % 4
     from_fwd = (y + step + 8) % 4
@@ -298,7 +285,6 @@
     def first_piece(h):
         weights_wait(0, h, quarter, core)
         relays = weights_copy(8, h, pgu, pd, quarter, core, (dp_z, mem), 0)
-        near_sends.extend(relays)
 
         @pl.when(near)
         def _():
@@ -326,21 +312,10 @@
         weights_wait(6, h, from_bwd, 1 - core)
         weights_wait(7, h, across, 1 - core)
 
-    stores = []
-
-    def store(src, dst, n):
-        copy = pltpu.make_async_copy(src, dst, out_sem.at[n])
-        copy.start()
-        stores.append(copy)
-
     def tokens(chunk):
-        slots_self(sg_v, ret_v, ret_self_sem, chunk).wait()
-        for i in range(1, 8):
-            slots_wait(sg_v, ret_v, rs_sem, rr_sem, chunk, i)
+        slots_wait(ret_v, rr_sem, chunk)
         for mb in (2 * chunk, 2 * chunk + 1):
             gin_v[mb] = lax.dot_general(mix_v[mb], ret_v[mb], TN, preferred_element_type=F32).astype(BF16)
-        half = pl.ds(2 * chunk, 2)
-        store(gin_v.at[half], gin_hbm.at[half], chunk)
 
     with jax.named_scope("hidden0"):
         hidden(0, wgu)
@@ -358,14 +333,10 @@
         second_piece(0)
     with jax.named_scope("w1b"):
         second_piece(1)
-    with jax.named_scope("w3a"):
-        third_piece(0)
     with jax.named_scope("slots0"):
         slots_arrive(0)
     with jax.named_scope("d_own0"):
         d_terms(0, 0, wd)
-    with jax.named_scope("w3b"):
-        third_piece(1)
     with jax.named_scope("slots1"):
         slots_arrive(1)
     with jax.named_scope("d_own1"):
@@ -373,6 +344,9 @@
     with jax.named_scope("weights0"):
         weight_terms(0, 0)
         weight_terms(0, 1)
+    with jax.named_scope("w3"):
+        third_piece(0)
+        third_piece(1)
     with jax.named_scope("ring_first0"):
         ring_first(0, 0)
         ring_first(0, 1)
@@ -384,24 +358,23 @@
     with jax.named_scope("d_partner"):
         d_terms(1, 0, pd)
         d_terms(1, 1, pd)
-    with jax.named_scope("ring_next0_1a"):
+    with jax.named_scope("weights1"):
+        weight_terms(1, 0)
+        weight_terms(1, 1)
+    with jax.named_scope("ring_next0_1"):
         ring_next(0, 0, 1)
+        ring_next(0, 1, 1)
     with jax.named_scope("slot_grads0"):
         slot_grads(0)
         start([slots_copy(sg_v, ret_v, rs_sem, rr_sem, 0, i) for i in range(1, 8)])
-        slots_self(sg_v, ret_v, ret_self_sem, 0).start()
-    with jax.named_scope("weights1"):
-        weight_terms(1, 0)
-        weight_terms(1, 1)
-    with jax.named_scope("ring_next0_1b"):
-        ring_next(0, 1, 1)
+        slots_self(sg_v, ret_v, rr_sem, 0).start()
+    with jax.named_scope("ring_first1"):
+        ring_first(1, 0)
+        ring_first(1, 1)
     with jax.named_scope("slot_grads1"):
         slot_grads(1)
         start([slots_copy(sg_v, ret_v, rs_sem, rr_sem, 1, i) for i in range(1, 8)])
-        slots_self(sg_v, ret_v, ret_self_sem, 1).start()
-    with jax.named_scope("ring_first1"):
-        ring_first(1, 0)
-        ring_first(1, 1)
+        slots_self(sg_v, ret_v, rr_sem, 1).start()
     with jax.named_scope("ring_next0_2"):
         ring_next(0, 0, 2)
         ring_next(0, 1, 2)
@@ -436,22 +409,26 @@
         total = total + zd[n].astype(F32)
     total = total * (1.0 / 128.0)
     down_v[...] = total[:, :256]
-    store(down_v, gd_hbm, 2)
     gate_v[...] = total[:, 256:512]
-    store(gate_v, gg_hbm, 3)
     up_v[...] = total[:, 512:]
-    store(up_v, gu_hbm, 4)
+
+    def left(ref, sem):
+        pltpu.make_async_copy(ref, ref, sem).wait()
 
     with jax.named_scope("wait_sends"):
-        for copy in sends:
-            copy.wait_send()
-        for copy in stores:
-            copy.wait()
+        left(s_send.at[:, pl.ds(0, 56)], ds_sem.at[0])
+        left(sg_v.at[:, pl.ds(0, 56)], rs_sem.at[0])
+        left(pgu.at[:, :, :, pl.ds(0, 56)], ws_sem.at[0, 0])
+        left(pd.at[:, :, :, :, pl.ds(0, 896)], ws_sem.at[0, 1])
+        left(drecv, cs_sem.at[0])
+        left(lsend, cs_sem.at[1])
+        left(ssend, cs_sem.at[2])
+        left(zd, cs_sem.at[3])
 
         @pl.when(near)
         def _():
-            for copy in near_sends:
-                copy.wait_send()
+            left(pgu.at[0, pl.ds(0, 2)], ws_sem.at[1, 0])
+            left(pd.at[0, pl.ds(0, 2)], ws_sem.at[1, 1])
 
 
 def per_device(grad_out, routes, route_probs, dispatched, w_gate, w_up, w_down):
@@ -464,14 +441,9 @@
     V = pltpu.VMEM
     results = pl.pallas_call(
         kernel,
-        out_shape=(
-            jax.ShapeDtypeStruct((4, 64, 1024), BF16),
-            jax.ShapeDtypeStruct((32, 256), F32),
-            jax.ShapeDtypeStruct((32, 256), F32),
-            jax.ShapeDtypeStruct((32, 256), F32),
-        ),
+        out_shape=(V((4, 64, 1024), BF16),) + (V((32, 256), F32),) * 3,
         in_specs=[hbm] * 7,
-        out_specs=(hbm,) * 4,
+        out_specs=(vmem,) * 4,
         scratch_shapes=[
             V((4, 8, 64), jnp.int32),
             V((4, 8, 64), BF16),
@@ -500,20 +472,23 @@
             V((32, 768), F32),
             V((2, 2, 32, 768), BF16),
             V((3, 32, 768), BF16),
-            V((4, 64, 1024), BF16),
-            V((32, 256), F32),
-            V((32, 256), F32),
-            V((32, 256), F32),
-            dma((6,)), dma((8,)), dma((5,)), dma((2,)), dma((2,)),
-            dma((2, 7)), dma((2, 7)), dma((2, 7)), dma((2, 7)),
-            dma((9, 2, 2)), dma((8, 2, 2)), dma((2, 2)), dma((2, 2)),
-            dma((2, 2, 4)), dma((2, 2, 4)), dma((2, 2, 3)), dma((2, 2, 3)), dma((3,)), dma((3,)),
+            dma((6,)), dma((1,)),
+            dma((1,)), dma((2,)), dma((1,)), dma((2,)),
+            dma((2, 2)), dma((8, 2, 2)), dma((4,)), dma((2, 2)),
+            dma((2, 2, 4)), dma((2, 2, 3)), dma((3,)),
         ],
         compiler_params=pltpu.CompilerParams(
-            collective_id=0, has_side_effects=True, vmem_limit_bytes=62000000
+            collective_id=0, has_side_effects=True, vmem_limit_bytes=48000000
         ),
         name="moe_backward",
-    )(grad_out, jnp.swapaxes(routes, 1, 2), jnp.swapaxes(route_probs, 1, 2), dispatched, wg, wu, wd)
+    )(
+        *(
+            pltpu.with_memory_space_constraint(a, pltpu.HBM)
+            for a in (
+                grad_out, jnp.swapaxes(routes, 1, 2), jnp.swapaxes(route_probs, 1, 2), dispatched, wg, wu, wd
+            )
+        )
+    )
 
     def store(a, b, c, d, out_a, out_b, out_c, out_d, sem):
         copies = [
@@ -531,6 +506,7 @@
         in_specs=[vmem] * 4,
         out_specs=(hbm,) * 4,
         scratch_shapes=[dma((4,))],
+        compiler_params=pltpu.CompilerParams(vmem_limit_bytes=1000000),
         name="store_results",
     )(*results)
 

time: 66.8 us -> 60 us (0.90)
  Pallas kernels: 66 us -> 59.1 us
    pallas_call x1, Pallas kernels: 64.1 us -> 58.3 us  [per_device(): pl.pallas_call(kernel, out_shape=(V((4, 64, 1024), BF16),) + (V((32, 256)...]
    pallas_call x1, Pallas kernels: 1.91 us -> 0.85 us  [per_device(): pl.pallas_call(store, out_shape=tuple((jax.ShapeDtypeStruct(r.shape, r.dt...]
where the time goes in v3:
time: 60 us; the launch traced here: 59.8 us
  Pallas kernels  59.1 us (98%)
  between operations  0.64 us (1%)
    pallas_call x1, Pallas kernels, per_device(): pl.pallas_call(kernel, out_shape=(V((4, 64, 1024), BF16),) + (V((32, 256)...  58.3 us

profile of v3, /device:TPU:8, one launch (start us, length us, event | category | flops | bytes accessed | tf_op | source)
XLA Modules:
  0.0 59.8 jit_solution(16026318492706375100)
XLA Ops:
  0.6 58.3 %moe_backward.1 = (bf16[4,64,1024]{2,1,0:T(8,128)(2,1)S(1)}, f32[32,256]{1,0:T(8,128)S(1)}, f32[32,256]{1,0:T(8,128)S(1)}, f32[32,256]{1,0:T(8,128)S(1)}) custom-call(bf16[4,64,1024]{2,1,0:T(8,128)(2,1)} %dy_hbm.1, s32[4,8,64]{2,1,0:T(8,128)} %bitcast.8, bf16[4,8,64]{2,1,0:T(8,128)(2,1)} %bitcast.9, bf16[4,128,1024]{2,1,0:T(8,128)(2,1)} %disp_hbm.1, ...), custom_call_target="tpu_custom_call" | custom-call | tf_op jit(solution)/shard_map/moe_backward/pallas_call | solution.py:442
  58.9 0.8 %store_results.1 = (bf16[4,64,1024]{2,1,0:T(8,128)(2,1)}, f32[32,256]{1,0:T(8,128)}, f32[32,256]{1,0:T(8,128)}, f32[32,256]{1,0:T(8,128)}) custom-call(bf16[4,64,1024]{2,1,0:T(8,128)(2,1)S(1)} %get-tuple-element.8.a, f32[32,256]{1,0:T(8,128)S(1)} %get-tuple-element.9.b, f32[32,256]{1,0:T(8,128)S(1)} %get-tuple-element.10.c, f32[32,256]{1,0:T(8,128)S(1)} %get-tuple-element.11.d), custom_call_target="tpu_custom_call" | custom-call | tf_op jit(solution)/shard_map/store_results/pallas_call | solution.py:503

commit v4 on v3

--- a/solution.py
+++ b/solution.py
@@ -18,7 +18,7 @@
     gin_v, gate_v, up_v, down_v,
     routes_v, probs_v, dy_v, x_v, wgu, wd, pgu, pd,
     mix_v, s_send, s_recv, act_v, fac_v, hid_v, dg_v, sg_v, ret_v,
-    rf, rb, drecv, lsend, lrecv, ssend, srecv, fin, finb, zd,
+    rf, rb, drecv, lsend, lrecv, ssend, srecv, fin, finb, zd, zsend, zrecv,
     in_sem, x_sem,
     ds_sem, dr_sem, rs_sem, rr_sem,
     ws_sem, wr_sem, cs_sem, cr_sem,
@@ -88,8 +88,20 @@
         for copy in weights_copy(n, h, pgu, pd, where, side, (dp_core, mem)):
             copy.wait_recv()
 
-    def pass_on(n, h, where, dev):
-        start(weights_copy(n, h, pgu, pd, where, core, dev))
+    def handle(n, h, where, onward):
+        held = weights_copy(n, h, pgu, pd, where, core, (dp_core, mem))
+        further = [weights_copy(to, h, pgu, pd, where, core, dev) for to, dev in onward]
+        relay = weights_copy(8, h, pgu, pd, where, core, (dp_z, mem), 0) if n == 0 else ()
+        for k in range(2):
+            held[k].wait_recv()
+            if n == 0:
+
+                @pl.when(near)
+                def _():
+                    relay[k].start()
+
+            for copies in further:
+                copies[k].start()
 
     near = (zl + zh) % 2 == 1
     far = (zl + zh) % 2 == 0
@@ -226,54 +238,92 @@
         lax.fori_loop(0, 2, body, 0)
         start([core_copy(half, s)])
 
+    is_far = (zl + zh + 1) % 2
+    full = pl.ds(0, 768)
+    downs = pl.ds(0, 256)
+    gates = pl.ds(256, 512)
+    streams = (
+        (0, is_far, full),
+        (0, 1 - is_far, downs),
+        (1, 0, full),
+        (1, 1, full),
+        (0, 1, gates),
+    )
+
     def core_copy(g, s):
         return remote(rb.at[g, s, :, 1 - core], drecv.at[g, s], cs_sem.at[0], cr_sem.at[g, s], (dp_core, mem))
 
-    def term(g, s, owner):
-        return rf[g, s, owner, core] + drecv[g, s, owner].astype(F32)
-
-    def long_copy(g, s, t):
-        at = (g, s, t)
-        return remote(lsend.at[at], lrecv.at[at], cs_sem.at[1], lsr_sem.at[at], (dp_fwd, mem))
-
-    def short_copy(g, s, t):
-        at = (g, s, t)
-        return remote(ssend.at[at], srecv.at[at], cs_sem.at[2], ssr_sem.at[at], (dp_bwd, mem))
-
-    def ring_first(g, s):
-        core_copy(g, s).wait_recv()
-        lsend[g, s, 0] = term(g, s, (y + 4) % 8).astype(BF16)
-        start([long_copy(g, s, 0)])
-        ssend[g, s, 0] = term(g, s, (y - 3 * step + 8) % 8).astype(BF16)
-        start([short_copy(g, s, 0)])
-
-    def ring_next(g, s, t):
-        own = term(g, s, (y + (4 - t) * step + 8) % 8)
-        long_copy(g, s, t - 1).wait_recv()
-        lsend[g, s, t] = (own + lrecv[g, s, t - 1].astype(F32)).astype(BF16)
-        start([long_copy(g, s, t)])
+    def term(n, owner):
+        g, s, cols = streams[n]
+        own = rf[g, s, owner, core, :, cols] + drecv[g, s, owner, :, cols].astype(F32)
+        if n == 4:
+            own = own + zrecv[owner].astype(F32)
+        return own
+
+    def at(ref, n, t):
+        g, s, cols = streams[n]
+        return ref.at[2 * g + s, t, :, cols]
+
+    group = (1, 2, 3, 3, 4)
+
+    def long_copy(n, t):
+        return remote(at(lsend, n, t), at(lrecv, n, t), cs_sem.at[group[n]], lsr_sem.at[n, t], (dp_fwd, mem))
+
+    def short_copy(n, t):
+        return remote(at(ssend, n, t), at(srecv, n, t), cs_sem.at[group[n] + 4], ssr_sem.at[n, t], (dp_bwd, mem))
+
+    def ring_first(n):
+        at(lsend, n, 0)[...] = term(n, (y + 4) % 8).astype(BF16)
+        start([long_copy(n, 0)])
+        at(ssend, n, 0)[...] = term(n, (y - 3 * step + 8) % 8).astype(BF16)
+        start([short_copy(n, 0)])
+
+    def ring_next(n, t):
+        own = term(n, (y + (4 - t) * step + 8) % 8)
+        long_copy(n, t - 1).wait_recv()
+        at(lsend, n, t)[...] = (own + at(lrecv, n, t - 1)[...].astype(F32)).astype(BF16)
+        start([long_copy(n, t)])
         if t < 3:
-            own = term(g, s, (y - (3 - t) * step + 8) % 8)
-            short_copy(g, s, t - 1).wait_recv()
-            ssend[g, s, t] = (own + srecv[g, s, t - 1].astype(F32)).astype(BF16)
-            start([short_copy(g, s, t)])
-
-    def z_copy(g, s):
-        n = (0, None, 1, 2)[2 * g + s]
-        dev = ((dp_z, dp)[s], (mem, partner)[g])
-        return remote(finb.at[g, s], zd.at[n], cs_sem.at[3], zr_sem.at[n], dev)
-
-    def ring_last(g, s):
-        own = term(g, s, y)
-        short_copy(g, s, 2).wait_recv()
-        own = own + srecv[g, s, 2].astype(F32)
-        long_copy(g, s, 3).wait_recv()
-        own = own + lrecv[g, s, 3].astype(F32)
-        if g == 0 and s == 1:
-            fin[...] = own
+            own = term(n, (y - (3 - t) * step + 8) % 8)
+            short_copy(n, t - 1).wait_recv()
+            at(ssend, n, t)[...] = (own + at(srecv, n, t - 1)[...].astype(F32)).astype(BF16)
+            start([short_copy(n, t)])
+
+    def ring_total(n):
+        own = term(n, y)
+        short_copy(n, 2).wait_recv()
+        own = own + at(srecv, n, 2)[...].astype(F32)
+        long_copy(n, 3).wait_recv()
+        return own + at(lrecv, n, 3)[...].astype(F32)
+
+    def partner_copy(s):
+        return remote(finb.at[1 + s], zd.at[1 + s], cs_sem.at[9], zr_sem.at[1 + s], ((dp_z, dp)[s], partner))
+
+    def other_z_copy(cols):
+        return remote(finb.at[0, :, cols], zd.at[0, :, cols], cs_sem.at[10], zr_sem.at[0], (dp_z, mem))
+
+    def z_first():
+        return remote(zsend, zrecv, cs_sem.at[11], zr_sem.at[3], (dp_z, mem))
+
+    def ring_last(n):
+        if n in (2, 3):
+            finb[n - 1] = ring_total(n).astype(BF16)
+            start([partner_copy(n - 2)])
+        elif n == 4:
+            fin[:, gates] = ring_total(n)
         else:
-            finb[g, s] = own.astype(BF16)
-            start([z_copy(g, s)])
+            own = ring_total(n)
+            cols = streams[n][2]
+            sends_on, keeps = (near, far) if n == 0 else (far, near)
+
+            @pl.when(sends_on)
+            def _():
+                finb[0, :, cols] = own.astype(BF16)
+                other_z_copy(cols).start()
+
+            @pl.when(keeps)
+            def _():
+                fin[:, cols] = own
 
     def slots_arrive(chunk):
         slots_wait(s_recv, dr_sem, chunk)
@@ -283,28 +333,14 @@
     across = (y + 2) % 4
 
     def first_piece(h):
-        weights_wait(0, h, quarter, core)
-        relays = weights_copy(8, h, pgu, pd, quarter, core, (dp_z, mem), 0)
-
-        @pl.when(near)
-        def _():
-            for copy in relays:
-                copy.start()
-
-        pass_on(1, h, quarter, (dp_fwd, mem))
-        pass_on(2, h, quarter, (dp_bwd, mem))
-        pass_on(4, h, quarter, (dp_core, mem))
+        handle(0, h, quarter, ((1, (dp_fwd, mem)), (2, (dp_bwd, mem)), (4, (dp_core, mem))))
 
     def second_piece(h):
-        weights_wait(1, h, from_bwd, core)
-        pass_on(3, h, from_bwd, (dp_fwd, mem))
-        pass_on(5, h, from_bwd, (dp_core, mem))
-        weights_wait(2, h, from_fwd, core)
-        pass_on(6, h, from_fwd, (dp_core, mem))
+        handle(1, h, from_bwd, ((3, (dp_fwd, mem)), (5, (dp_core, mem))))
+        handle(2, h, from_fwd, ((6, (dp_core, mem)),))
 
     def third_piece(h):
-        weights_wait(3, h, across, core)
-        pass_on(7, h, across, (dp_core, mem))
+        handle(3, h, across, ((7, (dp_core, mem)),))
 
     def last_piece(h):
         weights_wait(4, h, quarter, 1 - core)
@@ -347,14 +383,23 @@
     with jax.named_scope("w3"):
         third_piece(0)
         third_piece(1)
-    with jax.named_scope("ring_first0"):
-        ring_first(0, 0)
-        ring_first(0, 1)
     with jax.named_scope("wlast"):
         last_piece(0)
         last_piece(1)
     with jax.named_scope("hidden1"):
         hidden(1, pgu)
+    with jax.named_scope("ring_first0"):
+        core_copy(0, 0).wait_recv()
+        core_copy(0, 1).wait_recv()
+        ring_first(0)
+
+    @pl.when(far)
+    def _():
+        zsend[...] = (rf[0, 0, :, core, :, gates] + drecv[0, 0, :, :, gates].astype(F32)).astype(BF16)
+        z_first().start()
+
+    with jax.named_scope("ring_first0b"):
+        ring_first(1)
     with jax.named_scope("d_partner"):
         d_terms(1, 0, pd)
         d_terms(1, 1, pd)
@@ -362,48 +407,78 @@
         weight_terms(1, 0)
         weight_terms(1, 1)
     with jax.named_scope("ring_next0_1"):
-        ring_next(0, 0, 1)
-        ring_next(0, 1, 1)
+        ring_next(0, 1)
+        ring_next(1, 1)
     with jax.named_scope("slot_grads0"):
         slot_grads(0)
         start([slots_copy(sg_v, ret_v, rs_sem, rr_sem, 0, i) for i in range(1, 8)])
         slots_self(sg_v, ret_v, rr_sem, 0).start()
     with jax.named_scope("ring_first1"):
-        ring_first(1, 0)
-        ring_first(1, 1)
+        for s in range(2):
+            core_copy(1, s).wait_recv()
+            ring_first(2 + s)
     with jax.named_scope("slot_grads1"):
         slot_grads(1)
         start([slots_copy(sg_v, ret_v, rs_sem, rr_sem, 1, i) for i in range(1, 8)])
         slots_self(sg_v, ret_v, rr_sem, 1).start()
     with jax.named_scope("ring_next0_2"):
-        ring_next(0, 0, 2)
-        ring_next(0, 1, 2)
+        ring_next(0, 2)
+        ring_next(1, 2)
     with jax.named_scope("ring_next1_1"):
-        ring_next(1, 0, 1)
-        ring_next(1, 1, 1)
+        ring_next(2, 1)
+        ring_next(3, 1)
     with jax.named_scope("ring_next0_3"):
-        ring_next(0, 0, 3)
-        ring_next(0, 1, 3)
+        ring_next(0, 3)
+        ring_next(1, 3)
     with jax.named_scope("ring_next1_2"):
-        ring_next(1, 0, 2)
-        ring_next(1, 1, 2)
+        ring_next(2, 2)
+        ring_next(3, 2)
     with jax.named_scope("ring_last0"):
-        ring_last(0, 0)
-        ring_last(0, 1)
+        ring_last(0)
+        ring_last(1)
+
+    @pl.when(near)
+    def _():
+        z_first().wait_recv()
+        ring_first(4)
+
+    with jax.named_scope("ring_next1_3"):
+        ring_next(2, 3)
+        ring_next(3, 3)
+
+    @pl.when(near)
+    def _():
+        ring_next(4, 1)
+
+    with jax.named_scope("ring_last1"):
+        ring_last(2)
+        ring_last(3)
     with jax.named_scope("tokens0"):
         tokens(0)
-    with jax.named_scope("ring_next1_3"):
-        ring_next(1, 0, 3)
-        ring_next(1, 1, 3)
+
+    @pl.when(near)
+    def _():
+        ring_next(4, 2)
+
+
+    with jax.named_scope("late"):
+
+        @pl.when(near)
+        def _():
+            ring_next(4, 3)
+            ring_last(4)
+            zd[0, :, gates] = jnp.zeros((32, 512), BF16)
+            other_z_copy(downs).wait_recv()
+
+        @pl.when(far)
+        def _():
+            other_z_copy(full).wait_recv()
+
     with jax.named_scope("tokens1"):
         tokens(1)
-    with jax.named_scope("ring_last1"):
-        ring_last(1, 0)
-        ring_last(1, 1)
-
     with jax.named_scope("wait_z"):
-        for copy in (z_copy(0, 0), z_copy(1, 0), z_copy(1, 1)):
-            copy.wait_recv()
+        partner_copy(0).wait_recv()
+        partner_copy(1).wait_recv()
     total = fin[...]
     for n in range(3):
         total = total + zd[n].astype(F32)
@@ -421,14 +496,26 @@
         left(pgu.at[:, :, :, pl.ds(0, 56)], ws_sem.at[0, 0])
         left(pd.at[:, :, :, :, pl.ds(0, 896)], ws_sem.at[0, 1])
         left(drecv, cs_sem.at[0])
-        left(lsend, cs_sem.at[1])
-        left(ssend, cs_sem.at[2])
-        left(zd, cs_sem.at[3])
+        left(lsend.at[is_far], cs_sem.at[1])
+        left(ssend.at[is_far], cs_sem.at[5])
+        left(lsend.at[1 - is_far, :, :, downs], cs_sem.at[2])
+        left(ssend.at[1 - is_far, :, :, downs], cs_sem.at[6])
+        left(lsend.at[pl.ds(2, 2)], cs_sem.at[3])
+        left(ssend.at[pl.ds(2, 2)], cs_sem.at[7])
+        left(finb.at[pl.ds(1, 2)], cs_sem.at[9])
 
         @pl.when(near)
         def _():
             left(pgu.at[0, pl.ds(0, 2)], ws_sem.at[1, 0])
             left(pd.at[0, pl.ds(0, 2)], ws_sem.at[1, 1])
+            left(lsend.at[1, :, :, gates], cs_sem.at[4])
+            left(ssend.at[1, :, :, gates], cs_sem.at[8])
+            left(finb.at[0], cs_sem.at[10])
+
+        @pl.when(far)
+        def _():
+            left(finb.at[0, :, downs], cs_sem.at[10])
+            left(zsend, cs_sem.at[11])
 
 
 def per_device(grad_out, routes, route_probs, dispatched, w_gate, w_up, w_down):
@@ -465,17 +552,19 @@
             V((2, 2, 8, 2, 32, 768), F32),
             V((2, 2, 8, 2, 32, 768), BF16),
             V((2, 2, 8, 32, 768), BF16),
-            V((2, 2, 4, 32, 768), BF16),
-            V((2, 2, 4, 32, 768), BF16),
-            V((2, 2, 3, 32, 768), BF16),
-            V((2, 2, 3, 32, 768), BF16),
+            V((4, 4, 32, 768), BF16),
+            V((4, 4, 32, 768), BF16),
+            V((4, 3, 32, 768), BF16),
+            V((4, 3, 32, 768), BF16),
             V((32, 768), F32),
-            V((2, 2, 32, 768), BF16),
             V((3, 32, 768), BF16),
+            V((3, 32, 768), BF16),
+            V((8, 32, 512), BF16),
+            V((8, 32, 512), BF16),
             dma((6,)), dma((1,)),
             dma((1,)), dma((2,)), dma((1,)), dma((2,)),
-            dma((2, 2)), dma((8, 2, 2)), dma((4,)), dma((2, 2)),
-            dma((2, 2, 4)), dma((2, 2, 3)), dma((3,)),
+            dma((2, 2)), dma((8, 2, 2)), dma((12,)), dma((2, 2)),
+            dma((5, 4)), dma((5, 3)), dma((4,)),
         ],
         compiler_params=pltpu.CompilerParams(
             collective_id=0, has_side_effects=True, vmem_limit_bytes=48000000

time: 60 us -> 58.6 us (0.977)
  the two profiles are of different devices: /device:TPU:8 before, /device:TPU:1 now
where the time goes in v4:
time: 58.6 us; the launch traced here: 58.5 us
  Pallas kernels  57.8 us (99%)
  between operations  0.64 us (1%)
    pallas_call x1, Pallas kernels, per_device(): pl.pallas_call(kernel, out_shape=(V((4, 64, 1024), BF16),) + (V((32, 256)...  57 us

profile of v4, /device:TPU:1, one launch (start us, length us, event | category | flops | bytes accessed | tf_op | source)
XLA Modules:
  0.0 58.5 jit_solution(1845737306964893513)
XLA Ops:
  0.6 57.0 %moe_backward.1 = (bf16[4,64,1024]{2,1,0:T(8,128)(2,1)S(1)}, f32[32,256]{1,0:T(8,128)S(1)}, f32[32,256]{1,0:T(8,128)S(1)}, f32[32,256]{1,0:T(8,128)S(1)}) custom-call(bf16[4,64,1024]{2,1,0:T(8,128)(2,1)} %dy_hbm.1, s32[4,8,64]{2,1,0:T(8,128)} %bitcast.8, bf16[4,8,64]{2,1,0:T(8,128)(2,1)} %bitcast.9, bf16[4,128,1024]{2,1,0:T(8,128)(2,1)} %disp_hbm.1, ...), custom_call_target="tpu_custom_call" | custom-call | tf_op jit(solution)/shard_map/moe_backward/pallas_call | solution.py:529
  57.6 0.8 %store_results.1 = (bf16[4,64,1024]{2,1,0:T(8,128)(2,1)}, f32[32,256]{1,0:T(8,128)}, f32[32,256]{1,0:T(8,128)}, f32[32,256]{1,0:T(8,128)}) custom-call(bf16[4,64,1024]{2,1,0:T(8,128)(2,1)S(1)} %get-tuple-element.8.a, f32[32,256]{1,0:T(8,128)S(1)} %get-tuple-element.9.b, f32[32,256]{1,0:T(8,128)S(1)} %get-tuple-element.10.c, f32[32,256]{1,0:T(8,128)S(1)} %get-tuple-element.11.d), custom_call_target="tpu_custom_call" | custom-call | tf_op jit(solution)/shard_map/store_results/pallas_call | solution.py:592

commit v5 on v4

--- a/solution.py
+++ b/solution.py
@@ -406,13 +406,13 @@
     with jax.named_scope("weights1"):
         weight_terms(1, 0)
         weight_terms(1, 1)
-    with jax.named_scope("ring_next0_1"):
-        ring_next(0, 1)
-        ring_next(1, 1)
     with jax.named_scope("slot_grads0"):
         slot_grads(0)
         start([slots_copy(sg_v, ret_v, rs_sem, rr_sem, 0, i) for i in range(1, 8)])
         slots_self(sg_v, ret_v, rr_sem, 0).start()
+    with jax.named_scope("ring_next0_1"):
+        ring_next(0, 1)
+        ring_next(1, 1)
     with jax.named_scope("ring_first1"):
         for s in range(2):
             core_copy(1, s).wait_recv()

time: 58.6 us -> 59.8 us (1.020)
  the two profiles are of different devices: /device:TPU:1 before, /device:TPU:128 now
where the time goes in v5:
time: 59.8 us; the launch traced here: 59.6 us
  Pallas kernels  59 us (99%)
  between operations  0.64 us (1%)
    pallas_call x1, Pallas kernels, per_device(): pl.pallas_call(kernel, out_shape=(V((4, 64, 1024), BF16),) + (V((32, 256)...  58.1 us

profile of v5, /device:TPU:128, one launch (start us, length us, event | category | flops | bytes accessed | tf_op | source)
XLA Modules:
  0.0 59.6 jit_solution(645209646247473665)
XLA Ops:
  0.6 58.1 %moe_backward.1 = (bf16[4,64,1024]{2,1,0:T(8,128)(2,1)S(1)}, f32[32,256]{1,0:T(8,128)S(1)}, f32[32,256]{1,0:T(8,128)S(1)}, f32[32,256]{1,0:T(8,128)S(1)}) custom-call(bf16[4,64,1024]{2,1,0:T(8,128)(2,1)} %dy_hbm.1, s32[4,8,64]{2,1,0:T(8,128)} %bitcast.8, bf16[4,8,64]{2,1,0:T(8,128)(2,1)} %bitcast.9, bf16[4,128,1024]{2,1,0:T(8,128)(2,1)} %disp_hbm.1, ...), custom_call_target="tpu_custom_call" | custom-call | tf_op jit(solution)/shard_map/moe_backward/pallas_call | solution.py:529
  58.8 0.8 %store_results.1 = (bf16[4,64,1024]{2,1,0:T(8,128)(2,1)}, f32[32,256]{1,0:T(8,128)}, f32[32,256]{1,0:T(8,128)}, f32[32,256]{1,0:T(8,128)}) custom-call(bf16[4,64,1024]{2,1,0:T(8,128)(2,1)S(1)} %get-tuple-element.8.a, f32[32,256]{1,0:T(8,128)S(1)} %get-tuple-element.9.b, f32[32,256]{1,0:T(8,128)S(1)} %get-tuple-element.10.c, f32[32,256]{1,0:T(8,128)S(1)} %get-tuple-element.11.d), custom_call_target="tpu_custom_call" | custom-call | tf_op jit(solution)/shard_map/store_results/pallas_call | solution.py:592

commit v6 on v5

--- a/solution.py
+++ b/solution.py
@@ -406,10 +406,6 @@
     with jax.named_scope("weights1"):
         weight_terms(1, 0)
         weight_terms(1, 1)
-    with jax.named_scope("slot_grads0"):
-        slot_grads(0)
-        start([slots_copy(sg_v, ret_v, rs_sem, rr_sem, 0, i) for i in range(1, 8)])
-        slots_self(sg_v, ret_v, rr_sem, 0).start()
     with jax.named_scope("ring_next0_1"):
         ring_next(0, 1)
         ring_next(1, 1)
@@ -417,13 +413,17 @@
         for s in range(2):
             core_copy(1, s).wait_recv()
             ring_first(2 + s)
+    with jax.named_scope("slot_grads0"):
+        slot_grads(0)
+        start([slots_copy(sg_v, ret_v, rs_sem, rr_sem, 0, i) for i in range(1, 8)])
+        slots_self(sg_v, ret_v, rr_sem, 0).start()
+    with jax.named_scope("ring_next0_2"):
+        ring_next(0, 2)
+        ring_next(1, 2)
     with jax.named_scope("slot_grads1"):
         slot_grads(1)
         start([slots_copy(sg_v, ret_v, rs_sem, rr_sem, 1, i) for i in range(1, 8)])
         slots_self(sg_v, ret_v, rr_sem, 1).start()
-    with jax.named_scope("ring_next0_2"):
-        ring_next(0, 2)
-        ring_next(1, 2)
     with jax.named_scope("ring_next1_1"):
         ring_next(2, 1)
         ring_next(3, 1)

time: 59.8 us -> 58.2 us (0.973)
  the two profiles are of different devices: /device:TPU:128 before, /device:TPU:8 now
where the time goes in v6:
time: 58.2 us; the launch traced here: 58 us
  Pallas kernels  57.4 us (99%)
  between operations  0.64 us (1%)
    pallas_call x1, Pallas kernels, per_device(): pl.pallas_call(kernel, out_shape=(V((4, 64, 1024), BF16),) + (V((32, 256)...  56.5 us

profile of v6, /device:TPU:8, one launch (start us, length us, event | category | flops | bytes accessed | tf_op | source)
XLA Modules:
  0.0 58.0 jit_solution(996981329288080959)
XLA Ops:
  0.6 56.5 %moe_backward.1 = (bf16[4,64,1024]{2,1,0:T(8,128)(2,1)S(1)}, f32[32,256]{1,0:T(8,128)S(1)}, f32[32,256]{1,0:T(8,128)S(1)}, f32[32,256]{1,0:T(8,128)S(1)}) custom-call(bf16[4,64,1024]{2,1,0:T(8,128)(2,1)} %dy_hbm.1, s32[4,8,64]{2,1,0:T(8,128)} %bitcast.8, bf16[4,8,64]{2,1,0:T(8,128)(2,1)} %bitcast.9, bf16[4,128,1024]{2,1,0:T(8,128)(2,1)} %disp_hbm.1, ...), custom_call_target="tpu_custom_call" | custom-call | tf_op jit(solution)/shard_map/moe_backward/pallas_call | solution.py:529
  57.2 0.8 %store_results.1 = (bf16[4,64,1024]{2,1,0:T(8,128)(2,1)}, f32[32,256]{1,0:T(8,128)}, f32[32,256]{1,0:T(8,128)}, f32[32,256]{1,0:T(8,128)}) custom-call(bf16[4,64,1024]{2,1,0:T(8,128)(2,1)S(1)} %get-tuple-element.8.a, f32[32,256]{1,0:T(8,128)S(1)} %get-tuple-element.9.b, f32[32,256]{1,0:T(8,128)S(1)} %get-tuple-element.10.c, f32[32,256]{1,0:T(8,128)S(1)} %get-tuple-element.11.d), custom_call_target="tpu_custom_call" | custom-call | tf_op jit(solution)/shard_map/store_results/pallas_call | solution.py:592
